TPU v7x, 32 devices: a whole 2x2x4 slice. The times are simulated.
32 devices in a mesh: rep: 4 (over x, core), shard: 8 (over z, y).
Axes of the slice: x: 2, y: 2, z: 4, core: 2. Of those that a mesh axis runs over, the one named last changes fastest.
Arguments:
- tokens: bfloat16 [64, 512, 768], P(None, ('rep', 'shard')), may hold values from -6 to 6
- lengths: int32 [64], replicated, may hold values from 1 to 512, 20480 in all
- seq_order: int32 [64], replicated, may hold values from 0 to 63, each once
- w_query: bfloat16 [768, 768], P('shard'), may hold values from -0.21875 to 0.21875
- w_key: bfloat16 [768, 768], P('shard'), may hold values from -0.21875 to 0.21875
- w_value: bfloat16 [768, 768], P('shard'), may hold values from -0.21875 to 0.21875
- w_out: bfloat16 [768, 768], P('shard'), may hold values from -0.875 to 0.875
- b_query: bfloat16 [768], P('shard'), may hold values from -3 to 3
- b_value: bfloat16 [768], P('shard'), may hold values from -3 to 3
- b_out: bfloat16 [768], P('shard'), may hold values from -3 to 3
- ln1_gain: bfloat16 [768], P('shard'), may hold values from 0.5 to 1.5
- ln1_bias: bfloat16 [768], P('shard'), may hold values from -3 to 3
- w_up: bfloat16 [768, 3072], P('shard'), may hold values from -0.21875 to 0.21875
- b_up: bfloat16 [3072], P('shard'), may hold values from -3 to 3
- w_down: bfloat16 [3072, 768], P('shard'), may hold values from -0.109375 to 0.109375
- b_down: bfloat16 [768], P('shard'), may hold values from -3 to 3
- ln2_gain: bfloat16 [768], P('shard'), may hold values from 0.5 to 1.5
- ln2_bias: bfloat16 [768], P('shard'), may hold values from -3 to 3
- cotangent: bfloat16 [64, 512, 768], P(('rep', 'shard')), may hold values from -6 to 6
Outputs:
- outputs: bfloat16 [64, 512, 768], P(('rep', 'shard'))
- grad_tokens: bfloat16 [64, 512, 768], P(None, ('rep', 'shard'))
- grad_w_query: float32 [768, 768], P('shard')
- grad_w_key: float32 [768, 768], P('shard')
- grad_w_value: float32 [768, 768], P('shard')
- grad_w_out: float32 [768, 768], P('shard')
- grad_b_query: float32 [768], P('shard')
- grad_b_value: float32 [768], P('shard')
- grad_b_out: float32 [768], P('shard')
- grad_ln1_gain: float32 [768], P('shard')
- grad_ln1_bias: float32 [768], P('shard')
- grad_w_up: float32 [768, 3072], P('shard')
- grad_b_up: float32 [3072], P('shard')
- grad_w_down: float32 [3072, 768], P('shard')
- grad_b_down: float32 [768], P('shard')
- grad_ln2_gain: float32 [768], P('shard')
- grad_ln2_bias: float32 [768], P('shard')
Inputs may be any that keep to these rules, and one draw needn't show every extreme that they name: `lengths`: each sequence has 1 to 512 valid leading positions and some sequence has 512. `seq_order`: a permutation of the 64 sequences.
All inputs are finite; a program needn't handle non-finite values.
Results may differ from a plain program's by a relative error of at most 0.02.
Values may be sent and summed in bfloat16 or wider, within the bound.
A program may use at most 192 MiB of HBM per device.

v0:
```python
from functools import partial

import jax
import jax.numpy as jnp
from jax import lax
from jax.sharding import PartitionSpec as P

HEADS = 12


NEG_FILL = -1e30
EPS_NORM = 1e-12


def contract_rows(left, right):
    return lax.dot_general(
        left, right, (((0,), (0,)), ((), ())), preferred_element_type=jnp.float32
    )


def contract_cols(left, right):
    return lax.dot_general(
        left, right, (((1,), (1,)), ((), ())), preferred_element_type=jnp.float32
    )


def norm_stats(resid):
    row_mean = jnp.mean(resid, axis=-1, keepdims=True)
    centered = resid - row_mean
    variance = jnp.mean(centered * centered, axis=-1, keepdims=True)
    inv_std = lax.rsqrt(variance + EPS_NORM)
    return (centered * inv_std, inv_std)


def norm_back(grad_in, normed, inv_std, gain):
    scaled = grad_in * gain
    mean_grad = jnp.mean(scaled, axis=-1, keepdims=True)
    mean_cross = jnp.mean(scaled * normed, axis=-1, keepdims=True)
    return inv_std * (scaled - mean_grad - normed * mean_cross)


def exact_gelu(values):
    return jax.nn.gelu(values, approximate=False)


def split_heads(matrix, seq_count, seq_len, head_count):
    return (
        matrix.reshape(seq_count, seq_len, head_count, -1)
        .transpose(0, 2, 1, 3)
        .reshape(seq_count * head_count, seq_len, -1)
    )


def join_heads(stacked, seq_count, head_count):
    seq_len = stacked.shape[1]
    return (
        stacked.reshape(seq_count, head_count, seq_len, -1)
        .transpose(0, 2, 1, 3)
        .reshape(seq_count * seq_len, -1)
    )


def head_scores(queries, keys_low, key_mask, score_scale):
    scores = contract_cols(queries, keys_low) * score_scale
    return jnp.where(key_mask[None, :], scores, NEG_FILL)


def attend_forward(packed, score_scale):
    queries, keys_low, values_low, key_mask = packed
    scores = head_scores(queries, keys_low, key_mask, score_scale)
    row_max = jnp.max(scores, axis=-1, keepdims=True)
    row_total = jnp.sum(jnp.exp(scores - row_max), axis=-1, keepdims=True)
    log_total = row_max + jnp.log(row_total)
    attn_probs = jnp.exp(scores - log_total).astype(jnp.bfloat16)
    context = jnp.dot(attn_probs, values_low, preferred_element_type=jnp.float32)
    return (context.astype(jnp.bfloat16), log_total[:, 0])


def attend_backward(packed, score_scale):
    queries, keys_low, values_low, key_mask, log_total, grad_context = packed
    scores = head_scores(queries, keys_low, key_mask, score_scale)
    attn_probs = jnp.exp(scores - log_total[:, None])
    probs_low = attn_probs.astype(jnp.bfloat16)
    grad_value = contract_rows(probs_low, grad_context)
    grad_probs = contract_cols(grad_context, values_low)
    row_dot = jnp.sum(attn_probs * grad_probs, axis=-1, keepdims=True)
    grad_scores = (attn_probs * (grad_probs - row_dot)).astype(jnp.bfloat16)
    grad_query = jnp.dot(grad_scores, keys_low, preferred_element_type=jnp.float32) * score_scale
    grad_key = contract_rows(grad_scores, queries) * score_scale
    return (
        grad_query.astype(jnp.bfloat16),
        grad_key.astype(jnp.bfloat16),
        grad_value.astype(jnp.bfloat16),
    )


def per_device(
    tokens,
    lengths,
    seq_order,
    w_query,
    w_key,
    w_value,
    w_out,
    b_query,
    b_value,
    b_out,
    ln1_gain,
    ln1_bias,
    w_up,
    b_up,
    w_down,
    b_down,
    ln2_gain,
    ln2_bias,
    cotangent,
):
    device_count = lax.axis_size(("rep", "shard"))
    seq_count = cotangent.shape[0]
    seq_len = cotangent.shape[1]
    model_width = cotangent.shape[2]
    part_len = tokens.shape[1]
    head_count = HEADS
    score_scale = float(model_width // head_count) ** (-0.5)
    row_count = seq_count * seq_len
    slot_table = seq_order.reshape(device_count, seq_count).T
    picked = tokens[slot_table]
    arrived = lax.all_to_all(picked, ("rep", "shard"), split_axis=1, concat_axis=1, tiled=True)
    tok_rows = arrived.reshape(row_count, model_width)
    my_index = lax.axis_index(("rep", "shard"))
    my_slots = lax.dynamic_slice_in_dim(seq_order, my_index * seq_count, seq_count)
    my_lengths = lengths[my_slots]
    key_mask = jnp.arange(seq_len, dtype=jnp.int32)[None, :] < my_lengths[:, None]
    mask_items = jnp.repeat(key_mask, head_count, axis=0)
    valid_rows = key_mask.reshape(row_count, 1).astype(jnp.float32)
    attn_weights = (
        lax.all_gather(w_query, "shard", axis=0, tiled=True),
        lax.all_gather(w_key, "shard", axis=0, tiled=True),
        lax.all_gather(w_value, "shard", axis=0, tiled=True),
        lax.all_gather(w_out, "shard", axis=0, tiled=True),
        lax.all_gather(b_query, "shard", axis=0, tiled=True),
        lax.all_gather(b_value, "shard", axis=0, tiled=True),
        lax.all_gather(b_out, "shard", axis=0, tiled=True),
        lax.all_gather(ln1_gain, "shard", axis=0, tiled=True),
        lax.all_gather(ln1_bias, "shard", axis=0, tiled=True),
    )
    w_in = jnp.concatenate([attn_weights[0], attn_weights[1], attn_weights[2]], axis=1)
    projected = jnp.dot(tok_rows, w_in, preferred_element_type=jnp.float32)
    bias_query = attn_weights[4].astype(jnp.float32)
    bias_value = attn_weights[5].astype(jnp.float32)
    queries = (projected[:, :model_width] + bias_query).astype(jnp.bfloat16)
    keys_low = projected[:, model_width : 2 * model_width].astype(jnp.bfloat16)
    values_low = (projected[:, 2 * model_width :] + bias_value).astype(jnp.bfloat16)
    query_items = split_heads(queries, seq_count, seq_len, head_count)
    key_items = split_heads(keys_low, seq_count, seq_len, head_count)
    value_items = split_heads(values_low, seq_count, seq_len, head_count)
    context_items, log_totals = lax.map(
        partial(attend_forward, score_scale=score_scale),
        (query_items, key_items, value_items, mask_items),
    )
    context = join_heads(context_items, seq_count, head_count)
    attn_out = jnp.dot(context, attn_weights[3], preferred_element_type=jnp.float32) + attn_weights[
        6
    ].astype(jnp.float32)
    resid_one = tok_rows.astype(jnp.float32) + attn_out
    normed_one, inv_one = norm_stats(resid_one)
    gain_one = attn_weights[7].astype(jnp.float32)
    hidden_one = normed_one * gain_one + attn_weights[8].astype(jnp.float32)
    hidden_low = hidden_one.astype(jnp.bfloat16)
    ffn_weights = (
        lax.all_gather(w_up, "shard", axis=0, tiled=True),
        lax.all_gather(b_up, "shard", axis=0, tiled=True),
        lax.all_gather(w_down, "shard", axis=0, tiled=True),
        lax.all_gather(b_down, "shard", axis=0, tiled=True),
        lax.all_gather(ln2_gain, "shard", axis=0, tiled=True),
        lax.all_gather(ln2_bias, "shard", axis=0, tiled=True),
    )
    up_proj = jnp.dot(hidden_low, ffn_weights[0], preferred_element_type=jnp.float32) + ffn_weights[
        1
    ].astype(jnp.float32)
    activated, gelu_pull = jax.vjp(exact_gelu, up_proj)
    act_low = activated.astype(jnp.bfloat16)
    ffn_out = jnp.dot(act_low, ffn_weights[2], preferred_element_type=jnp.float32) + ffn_weights[
        3
    ].astype(jnp.float32)
    resid_two = hidden_one + ffn_out
    normed_two, inv_two = norm_stats(resid_two)
    gain_two = ffn_weights[4].astype(jnp.float32)
    result_rows = normed_two * gain_two + ffn_weights[5].astype(jnp.float32)
    outputs = result_rows.astype(jnp.bfloat16).reshape(seq_count, seq_len, model_width)
    grad_out = cotangent.reshape(row_count, model_width).astype(jnp.float32) * valid_rows
    d_ln2_gain = jnp.sum(grad_out * normed_two, axis=0)
    d_ln2_bias = jnp.sum(grad_out, axis=0)
    grad_resid_two = norm_back(grad_out, normed_two, inv_two, gain_two)
    grad_ffn = grad_resid_two.astype(jnp.bfloat16)
    ffn_again = (
        lax.all_gather(w_up, "shard", axis=0, tiled=True),
        lax.all_gather(b_up, "shard", axis=0, tiled=True),
        lax.all_gather(w_down, "shard", axis=0, tiled=True),
        lax.all_gather(b_down, "shard", axis=0, tiled=True),
        lax.all_gather(ln2_gain, "shard", axis=0, tiled=True),
        lax.all_gather(ln2_bias, "shard", axis=0, tiled=True),
    )
    d_w_down = contract_rows(act_low, grad_ffn)
    d_b_down = jnp.sum(grad_ffn.astype(jnp.float32), axis=0)
    grad_act = contract_cols(grad_ffn, ffn_again[2])
    grad_up = gelu_pull(grad_act)[0].astype(jnp.bfloat16)
    d_w_up = contract_rows(hidden_low, grad_up)
    d_b_up = jnp.sum(grad_up.astype(jnp.float32), axis=0)
    grad_hidden = grad_resid_two + contract_cols(grad_up, ffn_again[0])
    ffn_sums = (
        lax.psum_scatter(
            d_w_up.astype(jnp.bfloat16), "shard", scatter_dimension=0, tiled=True
        ).astype(jnp.float32),
        lax.psum_scatter(
            d_b_up.astype(jnp.bfloat16), "shard", scatter_dimension=0, tiled=True
        ).astype(jnp.float32),
        lax.psum_scatter(
            d_w_down.astype(jnp.bfloat16), "shard", scatter_dimension=0, tiled=True
        ).astype(jnp.float32),
        lax.psum_scatter(
            d_b_down.astype(jnp.bfloat16), "shard", scatter_dimension=0, tiled=True
        ).astype(jnp.float32),
        lax.psum_scatter(
            d_ln2_gain.astype(jnp.bfloat16), "shard", scatter_dimension=0, tiled=True
        ).astype(jnp.float32),
        lax.psum_scatter(
            d_ln2_bias.astype(jnp.bfloat16), "shard", scatter_dimension=0, tiled=True
        ).astype(jnp.float32),
    )
    d_ln1_gain = jnp.sum(grad_hidden * normed_one, axis=0)
    d_ln1_bias = jnp.sum(grad_hidden, axis=0)
    grad_resid_one = norm_back(grad_hidden, normed_one, inv_one, gain_one)
    grad_attn = grad_resid_one.astype(jnp.bfloat16)
    attn_again = (
        lax.all_gather(w_query, "shard", axis=0, tiled=True),
        lax.all_gather(w_key, "shard", axis=0, tiled=True),
        lax.all_gather(w_value, "shard", axis=0, tiled=True),
        lax.all_gather(w_out, "shard", axis=0, tiled=True),
        lax.all_gather(b_query, "shard", axis=0, tiled=True),
        lax.all_gather(b_value, "shard", axis=0, tiled=True),
        lax.all_gather(b_out, "shard", axis=0, tiled=True),
        lax.all_gather(ln1_gain, "shard", axis=0, tiled=True),
        lax.all_gather(ln1_bias, "shard", axis=0, tiled=True),
    )
    w_in_again = jnp.concatenate([attn_again[0], attn_again[1], attn_again[2]], axis=1)
    w_out_again = attn_again[3]
    d_w_out = contract_rows(context, grad_attn)
    d_b_out = jnp.sum(grad_attn.astype(jnp.float32), axis=0)
    grad_context = contract_cols(grad_attn, w_out_again).astype(jnp.bfloat16)
    grad_context_items = split_heads(grad_context, seq_count, seq_len, head_count)
    grad_q_items, grad_k_items, grad_v_items = lax.map(
        partial(attend_backward, score_scale=score_scale),
        (query_items, key_items, value_items, mask_items, log_totals, grad_context_items),
    )
    grad_q_rows = join_heads(grad_q_items, seq_count, head_count)
    grad_k_rows = join_heads(grad_k_items, seq_count, head_count)
    grad_v_rows = join_heads(grad_v_items, seq_count, head_count)
    grad_projected = jnp.concatenate([grad_q_rows, grad_k_rows, grad_v_rows], axis=1)
    d_w_in = contract_rows(tok_rows, grad_projected)
    d_w_query = d_w_in[:, :model_width]
    d_w_key = d_w_in[:, model_width : 2 * model_width]
    d_w_value = d_w_in[:, 2 * model_width :]
    d_b_query = jnp.sum(grad_q_rows.astype(jnp.float32), axis=0)
    d_b_value = jnp.sum(grad_v_rows.astype(jnp.float32), axis=0)
    grad_rows = grad_resid_one + contract_cols(grad_projected, w_in_again)
    attn_sums = (
        lax.psum_scatter(
            d_w_query.astype(jnp.bfloat16), "shard", scatter_dimension=0, tiled=True
        ).astype(jnp.float32),
        lax.psum_scatter(
            d_w_key.astype(jnp.bfloat16), "shard", scatter_dimension=0, tiled=True
        ).astype(jnp.float32),
        lax.psum_scatter(
            d_w_value.astype(jnp.bfloat16), "shard", scatter_dimension=0, tiled=True
        ).astype(jnp.float32),
        lax.psum_scatter(
            d_w_out.astype(jnp.bfloat16), "shard", scatter_dimension=0, tiled=True
        ).astype(jnp.float32),
        lax.psum_scatter(
            d_b_query.astype(jnp.bfloat16), "shard", scatter_dimension=0, tiled=True
        ).astype(jnp.float32),
        lax.psum_scatter(
            d_b_value.astype(jnp.bfloat16), "shard", scatter_dimension=0, tiled=True
        ).astype(jnp.float32),
        lax.psum_scatter(
            d_b_out.astype(jnp.bfloat16), "shard", scatter_dimension=0, tiled=True
        ).astype(jnp.float32),
        lax.psum_scatter(
            d_ln1_gain.astype(jnp.bfloat16), "shard", scatter_dimension=0, tiled=True
        ).astype(jnp.float32),
        lax.psum_scatter(
            d_ln1_bias.astype(jnp.bfloat16), "shard", scatter_dimension=0, tiled=True
        ).astype(jnp.float32),
    )
    back_rows = grad_rows.astype(jnp.bfloat16).reshape(
        seq_count, device_count, part_len, model_width
    )
    returned = lax.all_to_all(back_rows, ("rep", "shard"), split_axis=1, concat_axis=1, tiled=True)
    grad_tokens = jnp.zeros(tokens.shape, jnp.bfloat16).at[slot_table].set(returned)
    summed = (
        lax.psum(attn_sums[0].astype(jnp.bfloat16), "rep").astype(jnp.float32),
        lax.psum(attn_sums[1].astype(jnp.bfloat16), "rep").astype(jnp.float32),
        lax.psum(attn_sums[2].astype(jnp.bfloat16), "rep").astype(jnp.float32),
        lax.psum(attn_sums[3].astype(jnp.bfloat16), "rep").astype(jnp.float32),
        lax.psum(attn_sums[4].astype(jnp.bfloat16), "rep").astype(jnp.float32),
        lax.psum(attn_sums[5].astype(jnp.bfloat16), "rep").astype(jnp.float32),
        lax.psum(attn_sums[6].astype(jnp.bfloat16), "rep").astype(jnp.float32),
        lax.psum(attn_sums[7].astype(jnp.bfloat16), "rep").astype(jnp.float32),
        lax.psum(attn_sums[8].astype(jnp.bfloat16), "rep").astype(jnp.float32),
        lax.psum(ffn_sums[0].astype(jnp.bfloat16), "rep").astype(jnp.float32),
        lax.psum(ffn_sums[1].astype(jnp.bfloat16), "rep").astype(jnp.float32),
        lax.psum(ffn_sums[2].astype(jnp.bfloat16), "rep").astype(jnp.float32),
        lax.psum(ffn_sums[3].astype(jnp.bfloat16), "rep").astype(jnp.float32),
        lax.psum(ffn_sums[4].astype(jnp.bfloat16), "rep").astype(jnp.float32),
        lax.psum(ffn_sums[5].astype(jnp.bfloat16), "rep").astype(jnp.float32),
    )
    return (
        outputs,
        grad_tokens,
        summed[0],
        summed[1],
        summed[2],
        summed[3],
        summed[4],
        summed[5],
        summed[6],
        summed[7],
        summed[8],
        summed[9],
        summed[10],
        summed[11],
        summed[12],
        summed[13],
        summed[14],
    )


def solution(mesh):
    in_specs = (
        P(None, ("rep", "shard"), None),
        P(),
        P(),
        P("shard", None),
        P("shard", None),
        P("shard", None),
        P("shard", None),
        P("shard"),
        P("shard"),
        P("shard"),
        P("shard"),
        P("shard"),
        P("shard", None),
        P("shard"),
        P("shard", None),
        P("shard"),
        P("shard"),
        P("shard"),
        P(("rep", "shard"), None, None),
    )
    out_specs = (
        P(("rep", "shard"), None, None),
        P(None, ("rep", "shard"), None),
        P("shard", None),
        P("shard", None),
        P("shard", None),
        P("shard", None),
        P("shard"),
        P("shard"),
        P("shard"),
        P("shard"),
        P("shard"),
        P("shard", None),
        P("shard"),
        P("shard", None),
        P("shard"),
        P("shard"),
        P("shard"),
    )
    return jax.shard_map(
        per_device, mesh=mesh, in_specs=in_specs, out_specs=out_specs, check_vma=False
    )
```

profile of v0, /device:TPU:0, one launch (start us, length us, event | category | flops | bytes accessed | tf_op | source)
XLA Modules:
  0.0 1166.8 jit_solution(12780705168112768008)
XLA Ops:
  14.2 2.9 copy.93
  17.1 7.4 all-to-all-start
  28.1 69.5 %all-reduce.18 = (bf16[768]{0:T(1024)(128)(2,1)S(1)}, bf16[768]{0:T(1024)(128)(2,1)S(1)}, bf16[768]{0:T(1024)(128)(2,1)S(1)}, bf16[768]{0:T(1024)(128)(2,1)S(1)}...) all-reduce(bf16[768]{0:T(1024)(128)(2,1)S(1)} %dynamic-update-slice, ...), channel_id=1, replica_groups=mesh['rep'=4,'shard'=8] {'shard'}, use_global_device_ids=true, to_apply=%add | all-reduce | flops 5376 | bytes 21504
  98.4 26.0 %all-gather = bf16[8,1,384]{2,1,0:T(2,128)(2,1)S(1)} all-gather(bf16[1,1,384]{2,1,0:T(2,128)(2,1)S(1)} %reshape.295), channel_id=1, replica_groups=mesh['rep'=4,'shard'=8] {'shard'}, dimensions={0}, use_global_device_ids=true | all-gather | bytes 6912 | tf_op jit(solution)/shard_map/all_gather | solution.py:172
  125.8 2.4 constant_dynamic-update-slice_fusion.2
  128.2 2.4 constant_dynamic-update-slice_fusion.1
  130.6 21.8 %all-gather.12.cloned.1.call-done = bf16[768,768]{1,0:T(8,128)(2,1)} async-done(((bf16[96,768]{1,0:T(8,128)(2,1)}), bf16[768,768]{1,0:T(8,128)(2,1)}) %all-gather.12.cloned.1.call-update) | async-done | bytes 1179664 | tf_op jit(solution)/shard_map/all_gather | solution.py:139
  152.4 2.4 constant_dynamic-update-slice_fusion
  157.5 5.8 fusion.70
  163.5 2.3 fusion.50
  167.7 2.4 reshape.222
  170.1 5.4 copy.116
  177.2 2.4 reshape.226
  179.6 5.4 copy.118
  186.9 3.5 copy.117
  190.5 97.7 %while.26 = (s32[]{:T(128)}, bf16[24,512,64]{1,2,0:T(8,128)(2,1)S(1)}, f32[24,512]{1,0:T(8,128)}, pred[24,512]{1,0:T(8,128)(4,1)S(1)}, bf16[24,512,64]{2,1,0:T(8...) while((s32[]{:T(128)}, ...), condition=%wide.region_3.4_spmd, body=%wide.region_0.3_spmd.sunk | while | flops 68976128 | bytes 3626597 | solution.py:157
  291.4 3.9 fusion.67
  295.8 36.2 %multiply_convert_fusion.1 = (bf16[1024,3072]{1,0:T(8,128)(2,1)}, f32[1024,3072]{1,0:T(8,128)}, f32[1024,3072]{1,0:T(8,128)}) fusion(f32[3072]{0:T(1024)S(1)} %bitcast.222, bf16[768,3072]{1,0:T(8,128)(2,1)} %all-gather.16.cloned.1.call-done, f32[1024,768]{1,0:T(8,128)S(1)} %get-tuple-element.260, f32[768]{0:T(1024)S(1)} %convert_element_type.222, ...), kind=kOutput, calls=%fused_computation.64 | convolution fusion | flops 5043388416 | bytes 39348224 | tf_op jit(solution)/shard_map/dot_general | solution.py:178
  332.1 22.1 %all-gather.18.cloned.1.call-done = bf16[3072,768]{1,0:T(8,128)(2,1)} async-done(((bf16[384,768]{1,0:T(8,128)(2,1)}), bf16[3072,768]{1,0:T(8,128)(2,1)}) %all-gather.18.cloned.1.call-update) | async-done | bytes 4718608 | tf_op jit(solution)/shard_map/all_gather | solution.py:173
  354.2 9.8 fusion.68
  366.9 2.5 convert_reduce_fusion.1
  369.3 18.7 %fusion.69 = (bf16[3072]{0:T(1024)(128)(2,1)S(1)}, bf16[1024,3072]{1,0:T(8,128)(2,1)}) fusion(f32[1024,3072]{1,0:T(8,128)} %get-tuple-element.244, bf16[3072,768]{1,0:T(8,128)(2,1)} %all-gather.18.cloned.1.call-done, f32[1024,768]{1,0:T(8,128)} %get-tuple-element.240, f32[1024,3072]{1,0:T(8,128)} %get-tuple-element.261, f32[3072]{0:T(1024)S(1)} %bitcast.223), kind=kOutput, calls=%fused_computation.146 | convolution fusion | flops 4882953216 | bytes 39340032 | tf_op jit(solution)/shard_map/dot_general | solution.py:22
  388.1 11.0 multiply_reduce_fusion.2
  402.0 2.4 convolution_convert_fusion.6
  404.4 4.8 convolution_convert_fusion.5
  409.2 2.6 copy.105
  411.8 3.8 reshape.231
  415.6 5.4 copy.121
  425.0 235.1 %while.27 = (s32[]{:T(128)}, bf16[24,512,64]{1,2,0:T(8,128)(2,1)}, bf16[24,512,64]{1,2,0:T(8,128)(2,1)}, bf16[24,512,64]{1,2,0:T(8,128)(2,1)}, pred[24,512]{1,0:...) while((s32[]{:T(128)}, bf16[24,512,64]{1,2,0:T(8,128)(2,1)}, ...), condition=%wide.region_14.15_spmd, body=%wide.region_12.14_spmd.sunk | while | flops 170294784 | bytes 8995445 | solution.py:252
  660.1 3.1 copy.111
  665.7 3.0 copy.113
  670.7 4.2 convolution_convert_fusion.4
  678.2 9.9 convolution_convert_fusion.2
  688.2 10.5 convolution_convert_fusion.3
  698.7 8.2 add_convert_fusion.1
  708.3 3.4 all-to-all-start.1
  713.6 38.8 %reduce-scatter.11.cloned.1.call-done = bf16[96,768]{1,0:T(8,128)(2,1)} async-done(((bf16[768,768]{1,0:T(8,128)(2,1)}), bf16[96,768]{1,0:T(8,128)(2,1)}) %reduce-scatter.11.cloned.1.call-update) | async-done | bytes 147472 | tf_op jit(solution)/shard_map/reduce_scatter | solution.py:274
  752.4 67.3 %reduce-scatter.7.cloned.1.call-done = bf16[96,768]{1,0:T(8,128)(2,1)} async-done(((bf16[768,768]{1,0:T(8,128)(2,1)}), bf16[96,768]{1,0:T(8,128)(2,1)}) %reduce-scatter.7.cloned.1.call-update) | async-done | bytes 147472 | tf_op jit(solution)/shard_map/reduce_scatter | solution.py:268
  819.7 67.4 %reduce-scatter.9.cloned.1.call-done = bf16[96,768]{1,0:T(8,128)(2,1)} async-done(((bf16[768,768]{1,0:T(8,128)(2,1)}), bf16[96,768]{1,0:T(8,128)(2,1)}) %reduce-scatter.9.cloned.1.call-update) | async-done | bytes 147472 | tf_op jit(solution)/shard_map/reduce_scatter | solution.py:271
  887.2 98.3 %reduce-scatter.17.cloned.1.call-done = bf16[384,768]{1,0:T(8,128)(2,1)} async-done(((bf16[3072,768]{1,0:T(8,128)(2,1)}), bf16[384,768]{1,0:T(8,128)(2,1)}) %reduce-scatter.17.cloned.1.call-update) | async-done | bytes 589840 | tf_op jit(solution)/shard_map/reduce_scatter | solution.py:218
  985.5 98.8 %reduce-scatter.15.cloned.1.call-done = bf16[96,3072]{1,0:T(8,128)(2,1)} async-done(((bf16[768,3072]{1,0:T(8,128)(2,1)}), bf16[96,3072]{1,0:T(8,128)(2,1)}) %reduce-scatter.15.cloned.1.call-update) | async-done | bytes 589840 | tf_op jit(solution)/shard_map/reduce_scatter | solution.py:212
  1084.4 4.1 bitcast_reduce_fusion.1
  1088.5 4.1 bitcast_reduce_fusion
  1092.7 35.8 %all-reduce.17 = (bf16[768]{0:T(1024)(128)(2,1)S(1)}, bf16[768]{0:T(1024)(128)(2,1)S(1)}, bf16[768]{0:T(1024)(128)(2,1)S(1)}, bf16[768]{0:T(1024)(128)(2,1)S(1)}...) all-reduce(bf16[768]{0:T(1024)(128)(2,1)S(1)} %dynamic-update-slice, ...), channel_id=1, replica_groups=mesh['rep'=4,'shard'=8] {'shard'}, use_global_device_ids=true, to_apply=%add.7 | all-reduce | flops 9984 | bytes 39936
  1129.2 5.7 all-reduce.19
  1144.1 8.4 scatter_fusion
  1152.5 2.2 convert_element_type.254
  1154.7 2.2 convert_element_type.257
  (534 shorter events, 388.4 us)
Async XLA Ops:
  7.2 5.1 copy-start
  7.2 118.6 %all-gather.8.cloned.1.call-start = ((), (), s32[]{:S(2)}) async-start(), calls=%async_computation.8 | async-start | bytes 1327104 | tf_op jit(solution)/shard_map/all_gather | solution.py:137
  7.9 120.2 %all-gather.10.cloned.1.call-start = ((), (), s32[]{:S(2)}) async-start(), calls=%async_computation.9 | async-start | bytes 1327104 | tf_op jit(solution)/shard_map/all_gather | solution.py:138
  8.7 143.7 %all-gather.12.cloned.1.call-start = ((), (), s32[]{:S(2)}) async-start(), calls=%async_computation.10 | async-start | bytes 1327104 | tf_op jit(solution)/shard_map/all_gather | solution.py:139
  9.4 282.0 %all-gather.14.cloned.1.call-start = ((), (), s32[]{:S(2)}) async-start(), calls=%async_computation.11 | async-start | bytes 1327104 | tf_op jit(solution)/shard_map/all_gather | solution.py:140
  10.0 285.8 %all-gather.16.cloned.1.call-start = ((), (), s32[]{:S(2)}) async-start(), calls=%async_computation.12 | async-start | bytes 5308416 | tf_op jit(solution)/shard_map/all_gather | solution.py:171
  11.5 5.5 copy-start.19
  14.1 11.1 copy-start.21
  14.1 12.4 %copy-start.23 = (bf16[96]{0:T(256)(128)(2,1)S(1)}, bf16[96]{0:T(256)(128)(2,1)}, u32[]{:S(2)}) copy-start(bf16[96]{0:T(256)(128)(2,1)} %param.30) | copy-start | bytes 580
  14.1 12.6 %copy-start.24 = (bf16[96]{0:T(256)(128)(2,1)S(1)}, bf16[96]{0:T(256)(128)(2,1)}, u32[]{:S(2)}) copy-start(bf16[96]{0:T(256)(128)(2,1)} %param.31) | copy-start | bytes 580
  14.1 12.8 %copy-start.25 = (bf16[96]{0:T(256)(128)(2,1)S(1)}, bf16[96]{0:T(256)(128)(2,1)}, u32[]{:S(2)}) copy-start(bf16[96]{0:T(256)(128)(2,1)} %param.32) | copy-start | bytes 580
  14.1 13.1 %copy-start.26 = (bf16[96]{0:T(256)(128)(2,1)S(1)}, bf16[96]{0:T(256)(128)(2,1)}, u32[]{:S(2)}) copy-start(bf16[96]{0:T(256)(128)(2,1)} %param.33) | copy-start | bytes 580
  14.1 13.3 %copy-start.27 = (bf16[96]{0:T(256)(128)(2,1)S(1)}, bf16[96]{0:T(256)(128)(2,1)}, u32[]{:S(2)}) copy-start(bf16[96]{0:T(256)(128)(2,1)} %param.34) | copy-start | bytes 580
  14.1 13.5 %copy-start.28 = (bf16[96]{0:T(256)(128)(2,1)S(1)}, bf16[96]{0:T(256)(128)(2,1)}, u32[]{:S(2)}) copy-start(bf16[96]{0:T(256)(128)(2,1)} %param.38) | copy-start | bytes 580
  14.1 13.7 %copy-start.29 = (bf16[96]{0:T(256)(128)(2,1)S(1)}, bf16[96]{0:T(256)(128)(2,1)}, u32[]{:S(2)}) copy-start(bf16[96]{0:T(256)(128)(2,1)} %param.39) | copy-start | bytes 580
  14.1 83.5 %copy-start.2 = (s32[64]{0:T(128)S(1)}, s32[64]{0:T(128)}, u32[]{:S(2)}) copy-start(s32[64]{0:T(128)} %param.24) | copy-start | bytes 772
  14.1 84.3 %copy-start.22 = (bf16[384]{0:T(512)(128)(2,1)S(1)}, bf16[384]{0:T(512)(128)(2,1)}, u32[]{:S(2)}) copy-start(bf16[384]{0:T(512)(128)(2,1)} %param.36) | copy-start | bytes 2308
  14.2 110.4 %copy-start.3 = (bf16[2,512,768]{2,1,0:T(8,128)(2,1)S(1)}, bf16[2,512,768]{2,1,0:T(8,128)(2,1)}, u32[]{:S(2)}) copy-start(bf16[2,512,768]{2,1,0:T(8,128)(2,1)} %param.41) | copy-start | bytes 4718596
  17.1 137.7 %all-to-all-start = ((bf16[2,32,16,768]{3,2,0,1:T(8,128)(2,1)}), bf16[2,32,16,768]{3,2,0,1:T(8,128)(2,1)}, u32[]{:S(2)}, u32[]{:S(2)}) async-start(bf16[2,32,16,768]{3,2,0,1:T(8,128)(2,1)} %copy.93), calls=%async_computation | async-start | bytes 3145728 | tf_op jit(solution)/shard_map/all_to_all | solution.py:128
  24.5 329.7 %all-gather.18.cloned.1.call-start = ((), (), s32[]{:S(2)}) async-start(), calls=%async_computation.13 | async-start | bytes 5308416 | tf_op jit(solution)/shard_map/all_gather | solution.py:173
  25.1 688.5 %reduce-scatter.13.cloned.1.call-start = ((), (), s32[]{:S(2)}) async-start(), calls=%async_computation.17 | async-start | bytes 1327104 | tf_op jit(solution)/shard_map/reduce_scatter | solution.py:277
  156.3 1.2 copy-start.9
  288.2 3.2 copy-start.17
  295.3 36.8 %copy-start.5 = (f32[1024,768]{1,0:T(8,128)}, f32[1024,768]{1,0:T(8,128)S(1)}, u32[]{:S(2)}) copy-start(f32[1024,768]{1,0:T(8,128)S(1)} %get-tuple-element.260) | copy-start | bytes 9437188
  364.0 1.4 copy-start.4
  388.1 11.0 copy-start.6
  399.1 2.9 copy-start.11
  400.4 1.6 copy-start.8
  421.1 331.4 %reduce-scatter.11.cloned.1.call-start = ((), (), s32[]{:S(2)}) async-start(), calls=%async_computation.16 | async-start | bytes 1327104 | tf_op jit(solution)/shard_map/reduce_scatter | solution.py:274
  660.1 3.6 copy-start.7
  669.3 1.4 copy-start.10
  670.7 4.2 copy-start.12
  676.9 142.9 %reduce-scatter.7.cloned.1.call-start = ((), (), s32[]{:S(2)}) async-start(), calls=%async_computation.14 | async-start | bytes 1327104 | tf_op jit(solution)/shard_map/reduce_scatter | solution.py:268
  677.6 209.6 %reduce-scatter.9.cloned.1.call-start = ((), (), s32[]{:S(2)}) async-start(), calls=%async_computation.15 | async-start | bytes 1327104 | tf_op jit(solution)/shard_map/reduce_scatter | solution.py:271
  678.2 307.3 %reduce-scatter.17.cloned.1.call-start = ((), (), s32[]{:S(2)}) async-start(), calls=%async_computation.19 | async-start | bytes 5308416 | tf_op jit(solution)/shard_map/reduce_scatter | solution.py:218
  688.2 396.2 %reduce-scatter.15.cloned.1.call-start = ((), (), s32[]{:S(2)}) async-start(), calls=%async_computation.18 | async-start | bytes 5308416 | tf_op jit(solution)/shard_map/reduce_scatter | solution.py:212
  707.0 6.2 copy-start.30
  708.3 433.0 %all-to-all-start.1 = ((bf16[2,32,16,768]{3,2,0,1:T(8,128)(2,1)}), bf16[2,32,16,768]{3,2,0,1:T(8,128)(2,1)}, u32[]{:S(2)}, u32[]{:S(2)}) async-start(bf16[2,32,16,768]{3,2,0,1:T(8,128)(2,1)} %copy.114), calls=%async_computation.1 | async-start | bytes 3145728 | tf_op jit(solution)/shard_map/all_to_all | solution.py:299
  711.8 381.0 %copy-start.18 = (bf16[768]{0:T(1024)(128)(2,1)S(1)}, bf16[768]{0:T(1024)(128)(2,1)}, u32[]{:S(2)}) copy-start(bf16[768]{0:T(1024)(128)(2,1)} %get-tuple-element.171) | copy-start | bytes 4612
  711.8 440.7 %all-reduce.23.cloned.1.call-start = ((), (), s32[]{:S(2)}) async-start(), calls=%async_computation.20 | async-start | bytes 3538944 | tf_op jit(solution)/shard_map/psum | solution.py:302
  1141.3 2.8 copy-start.20
  1144.1 15.7 %copy-start.1 = (bf16[64,16,768]{2,1,0:T(8,128)(2,1)S(1)}, bf16[64,16,768]{2,1,0:T(8,128)(2,1)}, u32[]{:S(2)}) copy-start(bf16[64,16,768]{2,1,0:T(8,128)(2,1)} %param.23) | copy-start | bytes 4718596
  1152.5 4.4 copy-start.16
  1152.5 5.1 copy-start.15
  1152.5 5.9 copy-start.14
  1152.5 6.6 copy-start.13
Sparse Core Ops, SparseCore 0:
  10.2 59.5 all-gather.7
  71.9 38.3 all-gather.9
  112.5 39.8 all-gather.11
  154.4 39.7 all-gather.13
  196.3 78.4 all-gather.15
  276.8 77.3 all-gather.17
  421.2 63.2 reduce-scatter.12
  677.0 75.4 reduce-scatter.10
  756.4 63.2 reduce-scatter.6
  823.5 63.5 reduce-scatter.8
  890.8 94.6 reduce-scatter.16
  989.0 95.2 reduce-scatter.14
  1087.1 45.7 all-reduce.22
where the time goes:
time: 1180 us; the launch traced here: 1170 us
  waiting for transfers between devices  420 us (36%)
  matrix products  379 us (32%)
  local copies, waits for them, and re-layouts  158 us (13%)
  blocking collectives  137 us (12%)
  other arithmetic  43.5 us (4%)
  between operations  17 us (1%)
    dot_general x76, matrix products, contract_cols(): lax.dot_general(left, right, (((1,), (1,)), ((), ())), preferred_element_...  137 us
    dot_general x52, matrix products, contract_rows(): lax.dot_general(left, right, (((0,), (0,)), ((), ())), preferred_element_...  114 us
    unnamed x2, blocking collectives  105 us
    reduce_scatter x1, waiting for transfers between devices, per_device(): lax.psum_scatter(d_w_up.astype(jnp.bfloat16), 'shard', scatter_dimension=...  98.8 us
    reduce_scatter x1, waiting for transfers between devices, per_device(): lax.psum_scatter(d_w_down.astype(jnp.bfloat16), 'shard', scatter_dimensio...  98.3 us
    reduce_scatter x1, waiting for transfers between devices, per_device(): lax.psum_scatter(d_w_key.astype(jnp.bfloat16), 'shard', scatter_dimension...  67.4 us
    reduce_scatter x1, waiting for transfers between devices, per_device(): lax.psum_scatter(d_w_query.astype(jnp.bfloat16), 'shard', scatter_dimensi...  67.3 us
    dot_general x24, matrix products, attend_backward(): jnp.dot(grad_scores, keys_low, preferred_element_type=jnp.float32)  42.7 us
  transfers between devices with their start and end apart: 15, of which 7 were waited for; matrix products, arithmetic and copies ran while one was open for 43% of the time, Pallas kernels for 0%

commit v1 on v0

v1 whole, which is shorter than its diff:
```python
from functools import partial

import jax
import jax.numpy as jnp
from jax import lax
from jax.experimental import pallas as pl
from jax.experimental.pallas import tpu as pltpu
from jax.sharding import PartitionSpec as P

HEADS = 12
HEAD_DIM = 64
PAIR = 128
NEG_FILL = -1e30
EPS_NORM = 1e-12
LOG2E = 1.4426950408889634
MESH = pl.DeviceIdType.MESH


def contract_rows(left, right):
    return lax.dot_general(
        left, right, (((0,), (0,)), ((), ())), preferred_element_type=jnp.float32
    )


def contract_cols(left, right):
    return lax.dot_general(
        left, right, (((1,), (1,)), ((), ())), preferred_element_type=jnp.float32
    )


def norm_stats(resid):
    row_mean = jnp.mean(resid, axis=-1, keepdims=True)
    centered = resid - row_mean
    variance = jnp.mean(centered * centered, axis=-1, keepdims=True)
    inv_std = lax.rsqrt(variance + EPS_NORM)
    return (centered * inv_std, inv_std)


def norm_back(grad_in, normed, inv_std, gain):
    scaled = grad_in * gain
    mean_grad = jnp.mean(scaled, axis=-1, keepdims=True)
    mean_cross = jnp.mean(scaled * normed, axis=-1, keepdims=True)
    return inv_std * (scaled - mean_grad - normed * mean_cross)


def exact_gelu(values):
    return jax.nn.gelu(values, approximate=False)


def attend_forward_kernel(len_ref, q_ref, k_ref, v_ref, ctx_ref, probs_ref, *, scale):
    seq_len = q_ref.shape[0]
    valid = len_ref[pl.program_id(0)]
    key_pos = lax.broadcasted_iota(jnp.int32, (seq_len, PAIR), 0)
    fill = jnp.where(key_pos < valid, 0.0, NEG_FILL)[:, :1]
    first = lax.broadcasted_iota(jnp.int32, (seq_len, PAIR), 1) < HEAD_DIM
    queries = q_ref[...]
    keys = k_ref[...]
    values_t = v_ref[...].T
    parts = []
    for head in range(2):
        own = first if head == 0 else jnp.logical_not(first)
        head_keys = jnp.where(own, keys, jnp.zeros_like(keys))
        scores = lax.dot_general(head_keys, queries, (((1,), (1,)), ((), ())), preferred_element_type=jnp.float32)
        scaled = scores * (scale * LOG2E) + fill
        top = jnp.max(scaled, axis=0, keepdims=True)
        raised = jnp.exp2(scaled - top)
        total = jnp.sum(raised, axis=0, keepdims=True)
        probs = (raised * (1.0 / total)).astype(jnp.bfloat16)
        probs_ref[head] = probs
        parts.append(jnp.dot(values_t[head * HEAD_DIM : (head + 1) * HEAD_DIM], probs, preferred_element_type=jnp.float32))
    ctx_ref[...] = jnp.concatenate(parts, axis=0).T.astype(jnp.bfloat16)

def attend_forward(projected, lens, seq_count, seq_len, width, scale):
    pairs = width // PAIR
    grid_spec = pltpu.PrefetchScalarGridSpec(
        num_scalar_prefetch=1, grid=(seq_count, pairs),
        in_specs=[
            pl.BlockSpec((seq_len, PAIR), lambda s, h, n: (s, h)),
            pl.BlockSpec((seq_len, PAIR), lambda s, h, n: (s, pairs + h)),
            pl.BlockSpec((seq_len, PAIR), lambda s, h, n: (s, 2 * pairs + h)),
        ],
        out_specs=[
            pl.BlockSpec((seq_len, PAIR), lambda s, h, n: (s, h)),
            pl.BlockSpec((2, seq_len, seq_len), lambda s, h, n: (s * pairs + h, 0, 0)),
        ])
    return pl.pallas_call(
        partial(attend_forward_kernel, scale=scale), grid_spec=grid_spec,
        out_shape=[jax.ShapeDtypeStruct((seq_count * seq_len, width), jnp.bfloat16),
                   jax.ShapeDtypeStruct((seq_count * 2 * pairs, seq_len, seq_len), jnp.bfloat16)],
        compiler_params=pltpu.CompilerParams(dimension_semantics=("arbitrary", "arbitrary")),
        name="attend_forward",
    )(lens, projected, projected, projected)

def attend_backward_kernel(q_ref, k_ref, v_ref, gctx_ref, probs_ref, out_ref, *, scale):
    seq_len = q_ref.shape[0]
    width = out_ref.shape[1] // 3
    first = lax.broadcasted_iota(jnp.int32, (seq_len, PAIR), 1) < HEAD_DIM
    queries = q_ref[...]
    keys_t = k_ref[...].T
    values = v_ref[...]
    grad_ctx = gctx_ref[...]
    gq_parts, gk_parts, gv_parts = [], [], []
    for head in range(2):
        own = first if head == 0 else jnp.logical_not(first)
        head_values = jnp.where(own, values, jnp.zeros_like(values))
        probs_low = probs_ref[head]
        probs = probs_low.astype(jnp.float32)
        grad_probs = lax.dot_general(head_values, grad_ctx, (((1,), (1,)), ((), ())), preferred_element_type=jnp.float32)
        row_dot = jnp.sum(probs * grad_probs, axis=0, keepdims=True)
        grad_scores = (probs * (grad_probs - row_dot)).astype(jnp.bfloat16)
        gv_parts.append(jnp.dot(probs_low, grad_ctx, preferred_element_type=jnp.float32))
        gk_parts.append(jnp.dot(grad_scores, queries, preferred_element_type=jnp.float32))
        gq_parts.append(jnp.dot(keys_t[head * HEAD_DIM : (head + 1) * HEAD_DIM], grad_scores, preferred_element_type=jnp.float32))
    col = pl.multiple_of(pl.program_id(1) * PAIR, PAIR)
    out_ref[:, pl.ds(col, PAIR)] = (jnp.concatenate(gq_parts, axis=0).T * scale).astype(jnp.bfloat16)
    out_ref[:, pl.ds(width + col, PAIR)] = (jnp.where(first, gk_parts[0], gk_parts[1]) * scale).astype(jnp.bfloat16)
    out_ref[:, pl.ds(2 * width + col, PAIR)] = jnp.where(first, gv_parts[0], gv_parts[1]).astype(jnp.bfloat16)

def attend_backward(projected, grad_context, probs, seq_count, seq_len, width, scale):
    pairs = width // PAIR
    return pl.pallas_call(
        partial(attend_backward_kernel, scale=scale), grid=(seq_count, pairs),
        in_specs=[
            pl.BlockSpec((seq_len, PAIR), lambda s, h: (s, h)),
            pl.BlockSpec((seq_len, PAIR), lambda s, h: (s, pairs + h)),
            pl.BlockSpec((seq_len, PAIR), lambda s, h: (s, 2 * pairs + h)),
            pl.BlockSpec((seq_len, PAIR), lambda s, h: (s, h)),
            pl.BlockSpec((2, seq_len, seq_len), lambda s, h: (s * pairs + h, 0, 0)),
        ],
        out_specs=pl.BlockSpec((seq_len, 3 * width), lambda s, h: (s, 0)),
        out_shape=jax.ShapeDtypeStruct((seq_count * seq_len, 3 * width), jnp.bfloat16),
        compiler_params=pltpu.CompilerParams(dimension_semantics=("arbitrary", "arbitrary")),
        name="attend_backward",
    )(projected, projected, projected, grad_context, probs)


def gather_kernel(layout, z_count, *refs):
    count = len(layout)
    local = refs[:count]
    whole = refs[count : 2 * count]
    send_sem, recv_sem, own_sem = refs[2 * count :]
    rep = lax.axis_index("rep")
    shard = lax.axis_index("shard")
    z, y = shard // 2, shard % 2
    core = rep % 2
    side = (rep // 2) % 2
    peer_core = rep + 1 - 2 * core
    peer_side = rep + 2 - 4 * side
    peer_y = shard + 1 - 2 * y
    has_up, has_down = z + 1 < z_count, z > 0

    barrier = pltpu.get_barrier_semaphore()
    def greet(target, amount=1):
        pl.semaphore_signal(barrier, inc=amount, device_id=target, device_id_type=MESH)
    greet((peer_core, shard))
    greet((peer_side, shard))
    greet((rep, peer_y))
    @pl.when(has_up)
    def _():
        greet((rep, shard + 2))
    @pl.when(has_down)
    def _():
        greet((rep, shard - 2))
    pl.semaphore_wait(barrier, 3 + has_up.astype(jnp.int32) + has_down.astype(jnp.int32))

    def part(group, ref, first, shards, owner_core, owner_side):
        split, share, across = layout[group]
        index = owner_side * 2 + owner_core if across else owner_core
        start = pl.multiple_of(index * share, share)
        rows = pl.ds(first, shards)
        if split == "columns":
            return ref.at[rows, :, pl.ds(start, share)]
        if split == "rows":
            return ref.at[rows, pl.ds(start, share), :]
        return ref.at[rows]

    slot_y, slot_x, slot_own, slot_far = (2 * z_count + i * z_count for i in range(4))

    def copy(group, source, first, shards, owner_core, owner_side, slot, target):
        return pltpu.make_async_remote_copy(
            src_ref=part(group, source, first, shards, owner_core, owner_side),
            dst_ref=part(group, whole[group], first, shards, owner_core, owner_side),
            send_sem=send_sem.at[group, slot],
            recv_sem=recv_sem.at[group, slot],
            device_id=target,
            device_id_type=MESH,
        )

    def own_part(group):
        return part(group, local[group], 0, 1, core, side)

    def keep_own(group):
        return pltpu.make_async_copy(
            own_part(group), part(group, whole[group], shard, 1, core, side), own_sem.at[group]
        )

    def along(group, origin, distance, up):
        slot = (0 if up else z_count) + distance
        source = whole[group]
        if distance == 0:
            src = own_part(group)
        else:
            src = part(group, source, origin * 2 + y, 1, core, side)
        return pltpu.make_async_remote_copy(
            src_ref=src, dst_ref=part(group, whole[group], origin * 2 + y, 1, core, side),
            send_sem=send_sem.at[group, slot], recv_sem=recv_sem.at[group, slot],
            device_id=(rep, shard + 2 if up else shard - 2), device_id_type=MESH)

    def to_y(group, origin, own):
        if own:
            src = own_part(group)
        else:
            src = part(group, whole[group], origin * 2 + y, 1, core, side)
        return pltpu.make_async_remote_copy(
            src_ref=src, dst_ref=part(group, whole[group], origin * 2 + y, 1, core, side),
            send_sem=send_sem.at[group, slot_y + origin], recv_sem=recv_sem.at[group, slot_y + origin],
            device_id=(rep, peer_y), device_id_type=MESH)

    def from_y(group, origin):
        dst = part(group, whole[group], origin * 2 + 1 - y, 1, core, side)
        return pltpu.make_async_remote_copy(
            src_ref=dst, dst_ref=dst,
            send_sem=send_sem.at[group, slot_y + origin], recv_sem=recv_sem.at[group, slot_y + origin],
            device_id=(rep, peer_y), device_id_type=MESH)

    def to_x(group, origin, mine):
        return copy(group, whole[group], origin * 2, 2, core, side if mine else 1 - side, slot_x + origin, (peer_side, shard))

    def to_core(group, origin, mine_core, mine_side):
        return copy(group, whole[group], origin * 2, 2, core if mine_core else 1 - core, side if mine_side else 1 - side,
                    (slot_own if mine_side else slot_far) + origin, (peer_core, shard))

    steps = [(d, up) for d in range(1, z_count) for up in (True, False)]

    def valid(d, up):
        return z - d >= 0 if up else z + d < z_count

    for group in range(count):
        keep_own(group).start()
    for group in range(count):
        @pl.when(has_up)
        def _(group=group):
            along(group, z, 0, True).start()
        @pl.when(has_down)
        def _(group=group):
            along(group, z, 0, False).start()
        to_y(group, z, True).start()
    for group in range(count):
        keep_own(group).wait()

    def finish_pair(group, origin):
        from_y(group, origin).wait_recv()
        split, share, across = layout[group]
        if across:
            to_x(group, origin, True).start()
        if split is not None:
            to_core(group, origin, True, True).start()

    for group in range(count):
        across = layout[group][2]
        pending = []
        for d, up in steps:
            origin = z - d if up else z + d
            @pl.when(valid(d, up))
            def _(group=group, d=d, up=up, origin=origin):
                along(group, origin, d - 1, up).wait_recv()
                further = has_up if up else has_down
                if d < z_count - 1:
                    @pl.when(further)
                    def _():
                        along(group, origin, d, up).start()
                to_y(group, origin, False).start()
            if d == 1 and not up:
                finish_pair(group, z)
            if d > 1 and not up:
                for u in (True, False):
                    o = z - d + 1 if u else z + d - 1
                    @pl.when(valid(d - 1, u))
                    def _(group=group, o=o):
                        finish_pair(group, o)
        d = z_count - 1
        for u in (True, False):
            o = z - d if u else z + d
            @pl.when(valid(d, u))
            def _(group=group, o=o):
                finish_pair(group, o)

    order = [(0, True)] + steps
    def each(fn):
        for d, up in order:
            o = z - d if up else z + d
            if d == 0:
                fn(o)
            else:
                @pl.when(valid(d, up))
                def _(o=o):
                    fn(o)
    for group in range(count):
        if layout[group][2]:
            def relay(o, group=group):
                to_x(group, o, False).wait_recv()
                to_core(group, o, True, False).start()
            each(relay)
    for group in range(count):
        split, share, across = layout[group]
        def last(o, group=group, split=split, across=across):
            if split is not None:
                to_core(group, o, False, True).wait_recv()
            if across:
                to_core(group, o, False, False).wait_recv()
        each(last)
    for group in range(count):
        split, share, across = layout[group]
        @pl.when(has_up)
        def _(group=group):
            along(group, z, 0, True).wait_send()
        @pl.when(has_down)
        def _(group=group):
            along(group, z, 0, False).wait_send()
        for d, up in steps:
            if d < z_count - 1:
                origin = z - d if up else z + d
                @pl.when(jnp.logical_and(valid(d, up), has_up if up else has_down))
                def _(group=group, d=d, up=up, origin=origin):
                    along(group, origin, d, up).wait_send()
        def sent(o, group=group, split=split, across=across):
            to_y(group, o, False).wait_send()
            if across:
                to_x(group, o, True).wait_send()
                to_core(group, o, True, False).wait_send()
            if split is not None:
                to_core(group, o, True, True).wait_send()
        each(sent)

def gather_all(local, layout, shards, collective_id, cost=0):
    count = len(local)
    z_count = shards // 2
    slots = 6 * z_count
    return pl.pallas_call(
        partial(gather_kernel, layout, z_count),
        out_shape=[jax.ShapeDtypeStruct((shards,) + a.shape, a.dtype) for a in local],
        in_specs=[pl.BlockSpec(memory_space=pltpu.VMEM)] * count,
        out_specs=[pl.BlockSpec(memory_space=pl.ANY)] * count,
        scratch_shapes=[pltpu.SemaphoreType.DMA((count, slots)), pltpu.SemaphoreType.DMA((count, slots)), pltpu.SemaphoreType.DMA((count,))],
        compiler_params=pltpu.CompilerParams(collective_id=collective_id, has_side_effects=True),
        name="gather_weights",
        cost_estimate=pl.CostEstimate(flops=0, bytes_accessed=cost, transcendentals=0),
    )(*[a[None] for a in local])


def swap(value, bit):
    count = lax.axis_size("rep")
    return lax.ppermute(value, "rep", [(i, i ^ bit) for i in range(count)])


def pick(values, bit_value):
    return jnp.where(bit_value == 0, values[0], values[1])


def reduce_weight(pieces, core, side):
    shards = pieces[0][0].shape[0]
    both = jnp.stack([jnp.stack(pieces[0]), jnp.stack(pieces[1])])
    send = lax.dynamic_index_in_dim(both, 1 - core, 1, keepdims=False)
    keep = lax.dynamic_index_in_dim(both, core, 1, keepdims=False)
    arrived = swap(send, 1)
    far = 1 - side
    send = (
        lax.dynamic_index_in_dim(keep, far, 0, keepdims=False).astype(jnp.float32)
        + lax.dynamic_index_in_dim(arrived, far, 0, keepdims=False).astype(jnp.float32)
    ).astype(jnp.bfloat16)
    near = lax.dynamic_index_in_dim(keep, side, 0, keepdims=False).astype(
        jnp.float32
    ) + lax.dynamic_index_in_dim(arrived, side, 0, keepdims=False).astype(jnp.float32)
    summed = (near + swap(send, 2).astype(jnp.float32)).astype(jnp.bfloat16)
    spread = lax.all_to_all(summed, "shard", split_axis=0, concat_axis=0, tiled=True)
    total = jnp.sum(spread.astype(jnp.float32), axis=0).astype(jnp.bfloat16)
    bit = 4
    while bit < lax.axis_size("rep"):
        total = (total.astype(jnp.float32) + swap(total, bit).astype(jnp.float32)).astype(jnp.bfloat16)
        bit *= 2
    other_side = swap(total, 2)
    mine = jnp.stack([total, other_side])
    theirs = swap(mine, 1)
    by_core = [jnp.where(core == 0, mine, theirs), jnp.where(core == 0, theirs, mine)]
    quarters = []
    for s in range(2):
        for c in range(2):
            quarters.append(jnp.where(side == s, by_core[c][0], by_core[c][1]))
    return quarters


def by_columns(grad, shards):
    rows, columns = grad.shape
    quarter = columns // 4
    cut = [grad[:, i * quarter : (i + 1) * quarter].reshape(shards, rows // shards, quarter) for i in range(4)]
    return [[cut[0], cut[1]], [cut[2], cut[3]]]


def by_rows(grad, shards):
    rows, columns = grad.shape
    quarter = rows // shards // 4
    cut = grad.reshape(shards, 4, quarter, columns)
    return [[cut[:, 0], cut[:, 1]], [cut[:, 2], cut[:, 3]]]


def per_device(
    tokens,
    lengths,
    seq_order,
    w_query,
    w_key,
    w_value,
    w_out,
    b_query,
    b_value,
    b_out,
    ln1_gain,
    ln1_bias,
    w_up,
    b_up,
    w_down,
    b_down,
    ln2_gain,
    ln2_bias,
    cotangent,
):
    device_count = lax.axis_size(("rep", "shard"))
    shards = lax.axis_size("shard")
    core = lax.axis_index("rep") % 2
    side = (lax.axis_index("rep") // 2) % 2
    seq_count, seq_len, model_width = cotangent.shape
    hidden_width = w_up.shape[1]
    part_len = tokens.shape[1]
    score_scale = float(model_width // HEADS) ** (-0.5)
    row_count = seq_count * seq_len
    slot_table = seq_order.reshape(device_count, seq_count).T
    picked = tokens[slot_table]
    arrived = lax.all_to_all(picked, ("rep", "shard"), split_axis=1, concat_axis=1, tiled=True)
    tok_rows = arrived.reshape(row_count, model_width)
    my_index = lax.axis_index(("rep", "shard"))
    my_slots = lax.dynamic_slice_in_dim(seq_order, my_index * seq_count, seq_count)
    my_lengths = lengths[my_slots]
    key_mask = jnp.arange(seq_len, dtype=jnp.int32)[None, :] < my_lengths[:, None]
    valid_rows = key_mask.reshape(row_count, 1).astype(jnp.float32)

    w_attn = jnp.concatenate([w_query, w_key, w_value, w_out], axis=1)
    vectors = (b_query, b_value, b_out, ln1_gain, ln1_bias, b_down, ln2_gain, ln2_bias, b_up)
    packed = jnp.concatenate(vectors)
    room = 16 * PAIR
    packed = jnp.pad(packed, (0, room - packed.shape[0])).reshape(16, PAIR)
    layout = (
        ("columns", model_width, True),
        ("columns", hidden_width // 4, True),
        ("rows", w_down.shape[0] // 2, False),
        (None, 0, False),
    )
    all_attn, all_up, all_down, all_small = gather_all(
        (w_attn, w_up, w_down, packed), layout, shards, collective_id=1, cost=100 << 20
    )
    all_attn = all_attn.reshape(model_width, 4 * model_width)
    all_up = all_up.reshape(model_width, hidden_width)
    all_down = all_down.reshape(hidden_width, model_width)
    flat = all_small.reshape(shards, room).astype(jnp.float32)
    small = []
    at = 0
    for vector in vectors:
        size = vector.shape[0]
        small.append(flat[:, at : at + size].reshape(shards * size))
        at += size
    f_b_query, f_b_value, f_b_out, gain_one, f_ln1_bias, f_b_down, gain_two, f_ln2_bias, f_b_up = small

    w_in = all_attn[:, : 3 * model_width]
    w_out_all = all_attn[:, 3 * model_width :]
    bias_in = jnp.concatenate([f_b_query, jnp.zeros_like(f_b_query), f_b_value])
    projected = (jnp.dot(tok_rows, w_in, preferred_element_type=jnp.float32) + bias_in).astype(jnp.bfloat16)
    context, probs = attend_forward(projected, my_lengths, seq_count, seq_len, model_width, score_scale)
    attn_out = jnp.dot(context, w_out_all, preferred_element_type=jnp.float32) + f_b_out
    resid_one = tok_rows.astype(jnp.float32) + attn_out
    normed_one, inv_one = norm_stats(resid_one)
    hidden_one = normed_one * gain_one + f_ln1_bias
    hidden_low = hidden_one.astype(jnp.bfloat16)
    up_proj = jnp.dot(hidden_low, all_up, preferred_element_type=jnp.float32) + f_b_up
    activated, gelu_pull = jax.vjp(exact_gelu, up_proj)
    act_low = activated.astype(jnp.bfloat16)
    ffn_out = jnp.dot(act_low, all_down, preferred_element_type=jnp.float32) + f_b_down
    resid_two = hidden_one + ffn_out
    normed_two, inv_two = norm_stats(resid_two)
    result_rows = normed_two * gain_two + f_ln2_bias
    outputs = result_rows.astype(jnp.bfloat16).reshape(seq_count, seq_len, model_width)
    grad_out = cotangent.reshape(row_count, model_width).astype(jnp.float32) * valid_rows
    d_ln2_gain = jnp.sum(grad_out * normed_two, axis=0)
    d_ln2_bias = jnp.sum(grad_out, axis=0)
    grad_resid_two = norm_back(grad_out, normed_two, inv_two, gain_two)
    grad_ffn = grad_resid_two.astype(jnp.bfloat16)
    d_w_down = contract_rows(act_low, grad_ffn).astype(jnp.bfloat16)
    down_quarters = reduce_weight(by_rows(d_w_down, shards), core, side)
    d_b_down = jnp.sum(grad_ffn.astype(jnp.float32), axis=0)
    grad_act = contract_cols(grad_ffn, all_down)
    grad_up = gelu_pull(grad_act)[0].astype(jnp.bfloat16)
    d_w_up = contract_rows(hidden_low, grad_up).astype(jnp.bfloat16)
    up_quarters = reduce_weight(by_columns(d_w_up, shards), core, side)
    d_b_up = jnp.sum(grad_up.astype(jnp.float32), axis=0)
    grad_hidden = grad_resid_two + contract_cols(grad_up, all_up)
    d_ln1_gain = jnp.sum(grad_hidden * normed_one, axis=0)
    d_ln1_bias = jnp.sum(grad_hidden, axis=0)
    grad_resid_one = norm_back(grad_hidden, normed_one, inv_one, gain_one)
    grad_attn = grad_resid_one.astype(jnp.bfloat16)
    d_w_out = contract_rows(context, grad_attn).astype(jnp.bfloat16)
    d_b_out = jnp.sum(grad_attn.astype(jnp.float32), axis=0)
    grad_context = contract_cols(grad_attn, w_out_all).astype(jnp.bfloat16)
    grad_projected = attend_backward(projected, grad_context, probs, seq_count, seq_len, model_width, score_scale)
    grad_rows = grad_resid_one + contract_cols(grad_projected, w_in)
    back_rows = grad_rows.astype(jnp.bfloat16).reshape(seq_count, device_count, part_len, model_width)
    returned = lax.all_to_all(back_rows, ("rep", "shard"), split_axis=1, concat_axis=1, tiled=True)
    d_w_in = contract_rows(tok_rows, grad_projected).astype(jnp.bfloat16)
    attn_quarters = reduce_weight(
        by_columns(jnp.concatenate([d_w_in, d_w_out], axis=1), shards), core, side
    )
    grad_wide = grad_projected.astype(jnp.float32)
    d_b_query = jnp.sum(grad_wide[:, :model_width], axis=0)
    d_b_value = jnp.sum(grad_wide[:, 2 * model_width :], axis=0)
    d_small = (d_b_query, d_b_value, d_b_out, d_ln1_gain, d_ln1_bias, d_b_down, d_ln2_gain, d_ln2_bias, d_b_up)
    rows = jnp.concatenate([d.reshape(shards, -1) for d in d_small], axis=1)
    rows = jnp.pad(rows, ((0, 0), (0, room - rows.shape[1]))).reshape(shards, 16, PAIR)
    spread = lax.all_to_all(rows, "shard", split_axis=0, concat_axis=0, tiled=True)
    total = jnp.sum(spread, axis=0)
    bit = 1
    while bit < lax.axis_size("rep"):
        total = total + swap(total, bit)
        bit *= 2
    total = total.reshape(room)
    small_out = []
    at = 0
    for vector in vectors:
        size = vector.shape[0]
        small_out.append(total[at : at + size])
        at += size
    g_b_query, g_b_value, g_b_out, g_ln1_gain, g_ln1_bias, g_b_down, g_ln2_gain, g_ln2_bias, g_b_up = small_out

    every = jnp.arange(seq_order.shape[0], dtype=jnp.int32)
    slot_of = jnp.sum(jnp.where(seq_order[None, :] == every[:, None], every[None, :], 0), axis=1)
    by_slot = returned.transpose(1, 0, 2, 3).reshape(device_count * seq_count, part_len, model_width)
    grad_tokens = by_slot[slot_of]
    g_up = jnp.concatenate(up_quarters, axis=1).astype(jnp.float32)
    g_down = jnp.concatenate(down_quarters, axis=0).astype(jnp.float32)
    g_attn = [q.astype(jnp.float32) for q in attn_quarters]
    return (
        outputs,
        grad_tokens,
        *g_attn,
        g_b_query,
        g_b_value,
        g_b_out,
        g_ln1_gain,
        g_ln1_bias,
        g_up,
        g_b_up,
        g_down,
        g_b_down,
        g_ln2_gain,
        g_ln2_bias,
    )


def solution(mesh):
    in_specs = (
        P(None, ("rep", "shard"), None),
        P(),
        P(),
        P("shard", None),
        P("shard", None),
        P("shard", None),
        P("shard", None),
        P("shard"),
        P("shard"),
        P("shard"),
        P("shard"),
        P("shard"),
        P("shard", None),
        P("shard"),
        P("shard", None),
        P("shard"),
        P("shard"),
        P("shard"),
        P(("rep", "shard"), None, None),
    )
    out_specs = (
        P(("rep", "shard"), None, None),
        P(None, ("rep", "shard"), None),
        P("shard", None),
        P("shard", None),
        P("shard", None),
        P("shard", None),
        P("shard"),
        P("shard"),
        P("shard"),
        P("shard"),
        P("shard"),
        P("shard", None),
        P("shard"),
        P("shard", None),
        P("shard"),
        P("shard"),
        P("shard"),
    )
    return jax.shard_map(
        per_device, mesh=mesh, in_specs=in_specs, out_specs=out_specs, check_vma=False
    )
```

time: 1180 us -> 500 us (0.42)
  waiting for transfers between devices: 420 us -> 113 us
  matrix products: 379 us -> 116 us
  Pallas kernels: 0 us -> 145 us
  blocking collectives: 137 us -> 0 us
  local copies, waits for them, and re-layouts: 158 us -> 23.3 us
  starting transfers between devices: 11.4 us -> 41.7 us
  between operations: 17 us -> 1.96 us
    reduce_scatter x6 -> x0, waiting for transfers between devices: 371 us -> none  [the longest x1 98.8 us: per_device(): lax.psum_scatter(d_w_up.astype(jnp.bfloat16), 'shard', scatter_dimension=...]
    pallas_call x0 -> x3, Pallas kernels: none -> 145 us  [the longest x1 102 us: gather_all(): pl.pallas_call(partial(gather_kernel, layout, z_count), out_shape=[jax.Sh...]
    unnamed x2 -> x0, blocking collectives: 105 us -> none
    dot_general x76 -> x4, matrix products: 137 us -> 41.8 us  [contract_cols(): lax.dot_general(left, right, (((1,), (1,)), ((), ())), preferred_element_...]
    dot_general x52 -> x4, matrix products: 114 us -> 22.4 us  [contract_rows(): lax.dot_general(left, right, (((0,), (0,)), ((), ())), preferred_element_...]
    ppermute x0 -> x14, waiting for transfers between devices: none -> 77.9 us  [swap(): return lax.ppermute(value, 'rep', [(i, i ^ bit) for i in range(count)])]
    dot_general x52 -> x4, matrix products: 127 us -> 52 us  [the longest x1 35.6 us: per_device(): jnp.dot(hidden_low, all_up, preferred_element_type=jnp.float32) + f_b_up]
    all_gather x6 -> x0, waiting for transfers between devices: 43.9 us -> none  [the longest x1 22.1 us: per_device(): lax.all_gather(w_down, 'shard', axis=0, tiled=True)]
  transfers between devices with their start and end apart: 15 -> 20, of which waited for: 7 -> 9; matrix products, arithmetic and copies ran while one was open for 43% -> 14% of each run, Pallas kernels for 0% -> 26%
where the time goes in v1:
time: 500 us; the launch traced here: 490 us
  Pallas kernels  145 us (29%)
  matrix products  116 us (23%)
  waiting for transfers between devices  113 us (23%)
  other arithmetic  49 us (10%)
  starting transfers between devices  41.7 us (8%)
  local copies, waits for them, and re-layouts  23.3 us (5%)
    pallas_call x1, Pallas kernels, gather_all(): pl.pallas_call(partial(gather_kernel, layout, z_count), out_shape=[jax.Sh...  102 us
    ppermute x14, waiting for transfers between devices, swap(): return lax.ppermute(value, 'rep', [(i, i ^ bit) for i in range(count)])  77.9 us
    dot_general x4, matrix products, contract_cols(): lax.dot_general(left, right, (((1,), (1,)), ((), ())), preferred_element_...  41.8 us
    dot_general x1, matrix products, per_device(): jnp.dot(hidden_low, all_up, preferred_element_type=jnp.float32) + f_b_up  35.6 us
    pallas_call x1, Pallas kernels, attend_backward(): pl.pallas_call(partial(attend_backward_kernel, scale=scale), grid=(seq_co...  23.5 us
    dot_general x4, matrix products, contract_rows(): lax.dot_general(left, right, (((0,), (0,)), ((), ())), preferred_element_...  22.4 us
    pallas_call x1, Pallas kernels, attend_forward(): pl.pallas_call(partial(attend_forward_kernel, scale=scale), grid_spec=gri...  19.7 us
    all_to_all x3, waiting for transfers between devices, reduce_weight(): lax.all_to_all(summed, 'shard', split_axis=0, concat_axis=0, tiled=True)  17.7 us
  transfers between devices with their start and end apart: 20, of which 9 were waited for; matrix products, arithmetic and copies ran while one was open for 14% of the time, Pallas kernels for 26%

profile of v1, /device:TPU:0, one launch (start us, length us, event | category | flops | bytes accessed | tf_op | source)
XLA Modules:
  0.0 490.3 jit_solution(6192320696564074019)
XLA Ops:
  4.2 7.3 %all-to-all-start = ((bf16[2,32,16,768]{3,2,0,1:T(8,128)(2,1)}), bf16[2,32,16,768]{3,2,0,1:T(8,128)(2,1)S(1)}, u32[]{:S(2)}, u32[]{:S(2)}) async-start(bf16[2,32,16,768]{3,2,0,1:T(8,128)(2,1)} %copy.59), calls=%async_computation | async-start | bytes 3145728 | tf_op jit(solution)/shard_map/all_to_all | solution.py:438
  12.4 1.8 maximum_bitcast_fusion.6.refs_0_
  14.3 102.0 %gather_weights.1 = (bf16[8,96,3072]{2,1,0:T(8,128)(2,1)}, bf16[8,96,3072]{2,1,0:T(8,128)(2,1)}, bf16[8,384,768]{2,1,0:T(8,128)(2,1)}, bf16[8,16,128]{2,1,0:T(8,128)(2,1)}) custom-call(bf16[1,96,3072]{2,1,0:T(8,128)(2,1)} %maximum_bitcast_fusion.6.refs_0_, bf16[1,96,3072]{2,1,0:T(8,128)(2,1)} %bitcast.213, bf16[1,384,768]{2,1,0:T(8,128)(2,1)} %bitcast.214, ...), custom_call_target="tpu_custom_call" | custom-call | bytes 104857600 | tf_op jit(solution)/shard_map/gather_weights/pallas_call | solution.py:339
  121.4 7.5 %add_convert_fusion.1.q_ref.k_ref.v_ref = bf16[1024,2304]{1,0:T(8,128)(2,1)} fusion(bf16[1024,768]{1,0:T(8,128)(2,1)S(1)} %bitcast.202, f32[2304]{0:T(1024)S(1)} %pad_maximum_fusion.3, bf16[768,3072]{1,0:T(8,128)(2,1)} %bitcast.228), kind=kOutput, calls=%fused_computation.21 | convolution fusion | flops 3628597248 | bytes 9839616 | tf_op jit(solution)/shard_map/dot_general | solution.py:475
  128.8 19.7 %attend_forward.1 = (bf16[1024,768]{1,0:T(8,128)(2,1)}, bf16[24,512,512]{2,1,0:T(8,128)(2,1)}) custom-call(s32[2]{0:T(128)} %copy-done.28, bf16[1024,2304]{1,0:T(8,128)(2,1)} %add_convert_fusion.1.q_ref.k_ref.v_ref, bf16[1024,2304]{1,0:T(8,128)(2,1)} %add_convert_fusion.1.q_ref.k_ref.v_ref, bf16[1024,2304]{1,0:T(8,128)(2,1)} %add_convert_fusion.1.q_ref.k_ref.v_ref), custom_call_target="tpu_custom_call" | custom-call | tf_op jit(solution)/shard_map/attend_forward/pallas_call | solution.py:86
  148.5 3.5 fusion.57
  152.6 35.6 %multiply_convert_fusion = (bf16[1024,3072]{1,0:T(8,128)(2,1)S(1)}, f32[1024,3072]{1,0:T(8,128)}, f32[1024,3072]{1,0:T(8,128)}) fusion(f32[3072]{0:T(1024)S(1)} %add.234, bf16[768,3072]{1,0:T(8,128)(2,1)S(1)} %bitcast.235, f32[1024,768]{1,0:T(8,128)S(1)} %get-tuple-element.94, f32[768]{0:T(1024)S(1)} %add.231, f32[768]{0:T(1024)S(1)} %mul.154, ...), kind=kOutput, calls=%fused_computation.7 | convolution fusion | flops 5043388416 | bytes 39348224 | tf_op jit(solution)/shard_map/dot_general | solution.py:482
  188.2 5.5 %fusion.58 = (f32[1024]{0:T(1024)S(1)}, f32[1024,768]{1,0:T(8,128)S(1)}) fusion(f32[768]{0:T(1024)S(1)} %add.237, bf16[1024,3072]{1,0:T(8,128)(2,1)S(1)} %get-tuple-element.43, bf16[3072,768]{1,0:T(8,128)(2,1)S(1)} %bitcast.239, f32[768]{0:T(1024)S(1)} %add.231, f32[768]{0:T(1024)S(1)} %mul.154, f32[1024]{0:T(1024)S(1)} %add_rsqrt_fusion.1, ...), kind=kOutput, calls=%fused_computation.180 | convolution fusion | flops 4837342208 | bytes 17323008 | tf_op jit(solution)/shard_map/dot_general | solution.py:485
  194.2 1.5 multiply_reduce_fusion
  195.8 2.4 convert_reduce_fusion.1
  198.2 7.0 %convolution_convert_fusion = bf16[3072,768]{1,0:T(8,128)(2,1)} fusion(bf16[1024,3072]{1,0:T(8,128)(2,1)S(1)} %get-tuple-element.43, f32[1024,768]{1,0:T(8,128)S(1)} %get-tuple-element.40), kind=kOutput, calls=%fused_computation.40 | convolution fusion | flops 4834983936 | bytes 14155776 | tf_op jit(solution)/shard_map/dot_general | solution.py:20
  205.2 19.0 %convert_reduce_fusion = (f32[3072]{0:T(1024)S(1)}, bf16[1024,3072]{1,0:T(8,128)(2,1)}) fusion(f32[1024,3072]{1,0:T(8,128)} %get-tuple-element.44, bf16[3072,768]{1,0:T(8,128)(2,1)} %bitcast.236, f32[1024,768]{1,0:T(8,128)} %copy-done.19, f32[1024,3072]{1,0:T(8,128)} %get-tuple-element.95, f32[3072]{0:T(1024)S(1)} %add.234), kind=kOutput, calls=%fused_computation.5 | convolution fusion | flops 4886098944 | bytes 39346176 | tf_op jit(solution)/shard_map/dot_general | solution.py:26
  224.2 8.6 %convolution_convert_fusion.1 = bf16[768,3072]{1,0:T(8,128)(2,1)S(1)} fusion(bf16[1024,3072]{1,0:T(8,128)(2,1)} %get-tuple-element.100, f32[1024,768]{1,0:T(8,128)S(1)} %copy-done.14, f32[768]{0:T(1024)S(1)} %add.231, f32[768]{0:T(1024)S(1)} %mul.154, f32[1024]{0:T(1024)S(1)} %add_rsqrt_fusion.1, f32[1024]{0:T(1024)S(1)} %broadcast_multiply_fusion.4), kind=kOutput, calls=%fused_computation.41 | convolution fusion | flops 4838129664 | bytes 14170112 | tf_op jit(solution)/shard_map/dot_general | solution.py:20
  232.9 9.7 %multiply_reduce_fusion.1 = (f32[768]{0:T(1024)S(1)}, f32[1024]{0:T(1024)S(1)}, f32[1024]{0:T(1024)S(1)}, f32[768]{0:T(1024)S(1)}, f32[1024,768]{1,0:T(8,128)S(1)}) fusion(f32[1024,768]{1,0:T(8,128)S(1)} %copy-done.14, f32[1024]{0:T(1024)S(1)} %add_rsqrt_fusion.1, f32[1024]{0:T(1024)S(1)} %broadcast_multiply_fusion.4, f32[768]{0:T(1024)S(1)} %mul.154, ...), kind=kOutput, calls=%fused_computation.48 | convolution fusion | flops 4839698432 | bytes 20472832 | tf_op jit(solution)/shard_map/dot_general | solution.py:26
  244.7 1.8 fusion.13
  248.0 1.7 fusion.15
  253.0 4.8 convolution_convert_fusion.3.gctx_ref
  257.8 23.5 %attend_backward.1 = bf16[1024,2304]{1,0:T(8,128)(2,1)} custom-call(bf16[1024,2304]{1,0:T(8,128)(2,1)} %add_convert_fusion.1.q_ref.k_ref.v_ref, bf16[1024,2304]{1,0:T(8,128)(2,1)} %add_convert_fusion.1.q_ref.k_ref.v_ref, bf16[1024,2304]{1,0:T(8,128)(2,1)} %add_convert_fusion.1.q_ref.k_ref.v_ref, bf16[1024,768]{1,0:T(8,128)(2,1)} %convolution_convert_fusion.3.gctx_ref, ...), custom_call_target="tpu_custom_call" | custom-call | tf_op jit(solution)/shard_map/attend_backward/pallas_call | solution.py:121
  281.3 3.2 convert_element_type.262
  285.6 5.3 %convolution_convert_fusion.2 = bf16[768,2304]{1,0:T(8,128)(2,1)} fusion(bf16[1024,768]{1,0:T(8,128)(2,1)S(1)} %bitcast.204, bf16[1024,2304]{1,0:T(8,128)(2,1)S(1)} %copy-done.11), kind=kOutput, calls=%fused_computation.42 | convolution fusion | flops 3625648128 | bytes 9830400 | tf_op jit(solution)/shard_map/dot_general | solution.py:20
  292.5 3.2 fusion.18
  295.7 1.6 collective-permute-start.11
  298.0 4.0 all-to-all-start.3
  302.0 2.4 fusion.54
  306.9 1.6 maximum_bitcast_fusion.1
  308.5 1.6 maximum_bitcast_fusion
  310.1 13.8 %collective-permute-done.11 = bf16[8,96,768]{2,1,0:T(8,128)(2,1)S(1)} collective-permute-done((bf16[8,96,768]{2,1,0:T(8,128)(2,1)}, bf16[8,96,768]{2,1,0:T(8,128)(2,1)S(1)}, u32[]{:S(2)}, u32[]{:S(2)}) %collective-permute-start.11) | collective-permute-done | bytes 1179680 | tf_op jit(solution)/shard_map/ppermute | solution.py:353
  323.9 3.1 fusion.20
  326.9 4.0 all-to-all-start.5
  330.9 3.4 fusion.17
  334.3 1.9 fusion.21
  337.8 26.9 %collective-permute-done.7 = bf16[8,96,768]{2,1,0:T(8,128)(2,1)S(1)} collective-permute-done((bf16[8,96,768]{2,1,0:T(8,128)(2,1)S(1)}, bf16[8,96,768]{2,1,0:T(8,128)(2,1)S(1)}, u32[]{:S(2)}, u32[]{:S(2)}) %collective-permute-start.7) | collective-permute-done | bytes 1179680 | tf_op jit(solution)/shard_map/ppermute | solution.py:353
  364.7 3.1 fusion.23
  367.8 6.4 %all-to-all-start.4 = ((bf16[8,96,768]{2,1,0:T(8,128)(2,1)}), bf16[8,96,768]{2,1,0:T(8,128)(2,1)}, u32[]{:S(2)}, u32[]{:S(2)}) async-start(bf16[8,96,768]{2,1,0:T(8,128)(2,1)} %fusion.23), calls=%async_computation.4 | async-start | bytes 2359296 | tf_op jit(solution)/shard_map/all_to_all | solution.py:375
  374.2 2.0 fusion.24
  376.2 1.9 collective-permute-start.1
  378.1 25.5 %collective-permute-done.1 = bf16[8,96,768]{2,1,0:T(8,128)(2,1)S(1)} collective-permute-done((bf16[8,96,768]{2,1,0:T(8,128)(2,1)S(1)}, bf16[8,96,768]{2,1,0:T(8,128)(2,1)S(1)}, u32[]{:S(2)}, u32[]{:S(2)}) %collective-permute-start.1) | collective-permute-done | bytes 1179680 | tf_op jit(solution)/shard_map/ppermute | solution.py:353
  403.6 3.1 fusion.26
  406.7 5.7 %all-to-all-start.2 = ((bf16[8,96,768]{2,1,0:T(8,128)(2,1)}), bf16[8,96,768]{2,1,0:T(8,128)(2,1)S(1)}, u32[]{:S(2)}, u32[]{:S(2)}) async-start(bf16[8,96,768]{2,1,0:T(8,128)(2,1)} %fusion.26), calls=%async_computation.2 | async-start | bytes 2359296 | tf_op jit(solution)/shard_map/all_to_all | solution.py:375
  412.4 8.2 %add_convert_fusion.2 = bf16[1024,768]{1,0:T(8,128)(2,1)S(1)} fusion(f32[1024,768]{1,0:T(8,128)} %copy-done.17, bf16[1024,2304]{1,0:T(8,128)(2,1)} %attend_backward.1, bf16[768,3072]{1,0:T(8,128)(2,1)} %bitcast.231), kind=kOutput, calls=%fused_computation.50 | convolution fusion | flops 3625451520 | bytes 12976128 | tf_op jit(solution)/shard_map/dot_general | solution.py:26
  421.9 17.7 %all-to-all-done.2 = bf16[8,96,768]{2,1,0:T(8,128)(2,1)S(1)} async-done(((bf16[8,96,768]{2,1,0:T(8,128)(2,1)}), bf16[8,96,768]{2,1,0:T(8,128)(2,1)S(1)}, u32[]{:S(2)}, u32[]{:S(2)}) %all-to-all-start.2) | async-done | bytes 1179680 | tf_op jit(solution)/shard_map/all_to_all | solution.py:375
  440.7 3.6 all-to-all-start.1
  446.5 1.8 collective-permute-start.5
  448.2 7.0 %collective-permute-done.5 = f32[16,128]{1,0:T(8,128)S(1)} collective-permute-done((f32[16,128]{1,0:T(8,128)S(1)}, f32[16,128]{1,0:T(8,128)S(1)}, u32[]{:S(2)}, u32[]{:S(2)}) %collective-permute-start.5) | collective-permute-done | bytes 8224 | tf_op jit(solution)/shard_map/ppermute | solution.py:353
  457.8 1.8 collective-permute-start.12
  461.4 3.7 collective-permute-done.2
  465.8 17.3 %all-to-all-done.1 = bf16[2,32,16,768]{3,2,0,1:T(8,128)(2,1)S(1)} async-done(((bf16[2,32,16,768]{3,2,0,1:T(8,128)(2,1)}), bf16[2,32,16,768]{3,2,0,1:T(8,128)(2,1)S(1)}, u32[]{:S(2)}, u32[]{:S(2)}) %all-to-all-start.1) | async-done | bytes 1572896 | tf_op jit(solution)/shard_map/all_to_all | solution.py:514
  483.1 1.8 gather_fusion.2
  (206 shorter events, 38.9 us)
Async XLA Ops:
  2.7 8.9 %copy-start.29 = (bf16[384]{0:T(512)(128)(2,1)S(1)}, bf16[384]{0:T(512)(128)(2,1)}, u32[]{:S(2)}) copy-start(bf16[384]{0:T(512)(128)(2,1)} %param.32) | copy-start | bytes 2308
  2.8 8.9 %copy-start.30 = (bf16[96]{0:T(256)(128)(2,1)S(1)}, bf16[96]{0:T(256)(128)(2,1)}, u32[]{:S(2)}) copy-start(bf16[96]{0:T(256)(128)(2,1)} %param.26) | copy-start | bytes 580
  2.8 8.9 %copy-start.31 = (bf16[96]{0:T(256)(128)(2,1)S(1)}, bf16[96]{0:T(256)(128)(2,1)}, u32[]{:S(2)}) copy-start(bf16[96]{0:T(256)(128)(2,1)} %param.27) | copy-start | bytes 580
  2.8 8.9 %copy-start.32 = (bf16[96]{0:T(256)(128)(2,1)S(1)}, bf16[96]{0:T(256)(128)(2,1)}, u32[]{:S(2)}) copy-start(bf16[96]{0:T(256)(128)(2,1)} %param.28) | copy-start | bytes 580
  2.8 8.9 %copy-start.33 = (bf16[96]{0:T(256)(128)(2,1)S(1)}, bf16[96]{0:T(256)(128)(2,1)}, u32[]{:S(2)}) copy-start(bf16[96]{0:T(256)(128)(2,1)} %param.29) | copy-start | bytes 580
  2.8 8.9 %copy-start.34 = (bf16[96]{0:T(256)(128)(2,1)S(1)}, bf16[96]{0:T(256)(128)(2,1)}, u32[]{:S(2)}) copy-start(bf16[96]{0:T(256)(128)(2,1)} %param.30) | copy-start | bytes 580
  2.8 8.9 %copy-start.35 = (bf16[96]{0:T(256)(128)(2,1)S(1)}, bf16[96]{0:T(256)(128)(2,1)}, u32[]{:S(2)}) copy-start(bf16[96]{0:T(256)(128)(2,1)} %param.34) | copy-start | bytes 580
  2.8 8.9 %copy-start.36 = (bf16[96]{0:T(256)(128)(2,1)S(1)}, bf16[96]{0:T(256)(128)(2,1)}, u32[]{:S(2)}) copy-start(bf16[96]{0:T(256)(128)(2,1)} %param.35) | copy-start | bytes 580
  2.8 8.9 %copy-start.37 = (bf16[96]{0:T(256)(128)(2,1)S(1)}, bf16[96]{0:T(256)(128)(2,1)}, u32[]{:S(2)}) copy-start(bf16[96]{0:T(256)(128)(2,1)} %param.36) | copy-start | bytes 580
  2.8 9.6 %copy-start.24 = (bf16[96,768]{1,0:T(8,128)(2,1)S(1)}, bf16[96,768]{1,0:T(8,128)(2,1)}, u32[]{:S(2)}) copy-start(bf16[96,768]{1,0:T(8,128)(2,1)} %param.25) | copy-start | bytes 442372
  2.9 9.5 %copy-start.25 = (bf16[96,768]{1,0:T(8,128)(2,1)S(1)}, bf16[96,768]{1,0:T(8,128)(2,1)}, u32[]{:S(2)}) copy-start(bf16[96,768]{1,0:T(8,128)(2,1)} %param.24) | copy-start | bytes 442372
  4.2 113.4 %copy-start.38 = (s32[64]{0:T(128)S(1)}, s32[64]{0:T(128)}, u32[]{:S(2)}) copy-start(s32[64]{0:T(128)} %param.21) | copy-start | bytes 772
  4.2 113.5 %copy-start.2 = (s32[64]{0:T(128)S(1)}, s32[64]{0:T(128)}, u32[]{:S(2)}) copy-start(s32[64]{0:T(128)} %param.20) | copy-start | bytes 772
  4.2 114.3 %copy-start.12 = (bf16[2,512,768]{2,1,0:T(8,128)(2,1)S(1)}, bf16[2,512,768]{2,1,0:T(8,128)(2,1)}, u32[]{:S(2)}) copy-start(bf16[2,512,768]{2,1,0:T(8,128)(2,1)} %param.37) | copy-start | bytes 4718596
  4.2 115.8 %all-to-all-start = ((bf16[2,32,16,768]{3,2,0,1:T(8,128)(2,1)}), bf16[2,32,16,768]{3,2,0,1:T(8,128)(2,1)S(1)}, u32[]{:S(2)}, u32[]{:S(2)}) async-start(bf16[2,32,16,768]{3,2,0,1:T(8,128)(2,1)} %copy.59), calls=%async_computation | async-start | bytes 3145728 | tf_op jit(solution)/shard_map/all_to_all | solution.py:438
  118.4 10.4 %copy-start.28 = (s32[2]{0:T(128)}, s32[2]{0:T(128)S(1)}, u32[]{:S(2)}) copy-start(s32[2]{0:T(128)S(1)} %gather_fusion.1) | copy-start | bytes 28
  128.8 19.7 %copy-start.22 = (bf16[2,32,16,768]{3,2,1,0:T(8,128)(2,1)S(1)}, bf16[2,32,16,768]{3,2,1,0:T(8,128)(2,1)}, u32[]{:S(2)}) copy-start(bf16[2,32,16,768]{3,2,1,0:T(8,128)(2,1)} %copy-done.21) | copy-start | bytes 4718596
  148.5 39.7 %slice-start.4 = ((s8[4718592]{0:T(1024)(128)(4,1)}), s8[4194304]{0:T(1024)(128)(4,1)S(1)}, s32[]{:S(2)}) async-start(s8[4718592]{0:T(1024)(128)(4,1)} %bitcast.237), calls=%async_computation.10 | async-start | bytes 8388608
  152.0 36.2 %copy-start.13 = (f32[1024,768]{1,0:T(8,128)}, f32[1024,768]{1,0:T(8,128)S(1)}, u32[]{:S(2)}) copy-start(f32[1024,768]{1,0:T(8,128)S(1)} %get-tuple-element.94) | copy-start | bytes 9437188
  152.6 35.6 %slice-start.5 = ((s8[4718592]{0:T(1024)(128)(4,1)}), s8[524288]{0:T(1024)(128)(4,1)S(1)}, s32[]{:S(2)}) async-start(s8[4718592]{0:T(1024)(128)(4,1)} %bitcast.237), calls=%async_computation.11 | async-start | bytes 1048576
  198.2 7.0 %copy-start.19 = (f32[1024,768]{1,0:T(8,128)}, f32[1024,768]{1,0:T(8,128)S(1)}, u32[]{:S(2)}) copy-start(f32[1024,768]{1,0:T(8,128)S(1)} %get-tuple-element.40) | copy-start | bytes 9437188
  205.2 19.0 %copy-start.14 = (f32[1024,768]{1,0:T(8,128)S(1)}, f32[1024,768]{1,0:T(8,128)}, u32[]{:S(2)}) copy-start(f32[1024,768]{1,0:T(8,128)} %copy-done.13) | copy-start | bytes 9437188
  224.2 8.6 %copy-start.20 = (f32[1024,768]{1,0:T(8,128)S(1)}, f32[1024,768]{1,0:T(8,128)}, u32[]{:S(2)}) copy-start(f32[1024,768]{1,0:T(8,128)} %copy-done.19) | copy-start | bytes 9437188
  224.2 18.4 %slice-start = ((s8[4718592]{0:T(1024)(128)(4,1)}), s8[4194304]{0:T(1024)(128)(4,1)S(1)}, s32[]{:S(2)}) async-start(s8[4718592]{0:T(1024)(128)(4,1)} %bitcast.195), calls=%async_computation.6 | async-start | bytes 8388608
  232.8 9.8 %slice-start.1 = ((s8[4718592]{0:T(1024)(128)(4,1)}), s8[524288]{0:T(1024)(128)(4,1)S(1)}, s32[]{:S(2)}) async-start(s8[4718592]{0:T(1024)(128)(4,1)} %bitcast.195), calls=%async_computation.7 | async-start | bytes 1048576
  246.8 45.7 %collective-permute-start.10 = (bf16[2,8,96,768]{3,2,1,0:T(8,128)(2,1)}, bf16[2,8,96,768]{3,2,1,0:T(8,128)(2,1)}, u32[]{:S(2)}, u32[]{:S(2)}) collective-permute-start(bf16[2,8,96,768]{3,2,1,0:T(8,128)(2,1)} %fusion.13), channel_id=1, source_target_pairs={{0,8},{8,0},{16,24},{24,16},{1,9},{9,1},{17,25},{25,17},{2,10},{10... | collective-permute-start | bytes 7077896 | tf_op jit(solution)/shard_map/ppermute | solution.py:353
  250.4 83.9 %collective-permute-start.6 = (bf16[2,8,96,768]{3,2,1,0:T(8,128)(2,1)}, bf16[2,8,96,768]{3,2,1,0:T(8,128)(2,1)}, u32[]{:S(2)}, u32[]{:S(2)}) collective-permute-start(bf16[2,8,96,768]{3,2,1,0:T(8,128)(2,1)} %fusion.15), channel_id=1, source_target_pairs={{0,8},{8,0},{16,24},{24,16},{1,9},{9,1},{17,25},{25,17},{2,10},{10... | collective-permute-start | bytes 7077896 | tf_op jit(solution)/shard_map/ppermute | solution.py:353
  295.7 28.1 %collective-permute-start.11 = (bf16[8,96,768]{2,1,0:T(8,128)(2,1)}, bf16[8,96,768]{2,1,0:T(8,128)(2,1)S(1)}, u32[]{:S(2)}, u32[]{:S(2)}) collective-permute-start(bf16[8,96,768]{2,1,0:T(8,128)(2,1)} %fusion.18), channel_id=1, source_target_pairs={{0,16},{8,24},{16,0},{24,8},{1,17},{9,25},{17,1},{25,9},{2,18},{10... | collective-permute-start | bytes 3538952 | tf_op jit(solution)/shard_map/ppermute | solution.py:353
  298.0 29.0 %all-to-all-start.3 = ((f32[8,16,128]{2,1,0:T(8,128)}), f32[8,16,128]{2,1,0:T(8,128)}, u32[]{:S(2)}, u32[]{:S(2)}) async-start(f32[8,16,128]{2,1,0:T(8,128)} %bitcast.221), calls=%async_computation.3 | async-start | bytes 131072 | tf_op jit(solution)/shard_map/all_to_all | solution.py:525
  308.5 15.4 %copy-start.6 = (bf16[1,2,8,96,768]{4,3,2,1,0:T(8,128)(2,1)S(1)}, bf16[1,2,8,96,768]{4,3,2,1,0:T(8,128)(2,1)}, u32[]{:S(2)}) copy-start(bf16[1,2,8,96,768]{4,3,2,1,0:T(8,128)(2,1)} %copy-done.5) | copy-start | bytes 7077892
  308.5 15.4 %copy-start.8 = (bf16[1,2,8,96,768]{4,3,2,1,0:T(8,128)(2,1)S(1)}, bf16[1,2,8,96,768]{4,3,2,1,0:T(8,128)(2,1)}, u32[]{:S(2)}) copy-start(bf16[1,2,8,96,768]{4,3,2,1,0:T(8,128)(2,1)} %copy-done.7) | copy-start | bytes 7077892
  326.9 40.8 %all-to-all-start.5 = ((bf16[8,96,768]{2,1,0:T(8,128)(2,1)}), bf16[8,96,768]{2,1,0:T(8,128)(2,1)S(1)}, u32[]{:S(2)}, u32[]{:S(2)}) async-start(bf16[8,96,768]{2,1,0:T(8,128)(2,1)} %fusion.20), calls=%async_computation.5 | async-start | bytes 2359296 | tf_op jit(solution)/shard_map/all_to_all | solution.py:375
  334.3 39.9 %collective-permute-start = (bf16[2,8,96,768]{3,2,1,0:T(8,128)(2,1)}, bf16[2,8,96,768]{3,2,1,0:T(8,128)(2,1)}, u32[]{:S(2)}, u32[]{:S(2)}) collective-permute-start(bf16[2,8,96,768]{3,2,1,0:T(8,128)(2,1)} %fusion.17), channel_id=1, source_target_pairs={{0,8},{8,0},{16,24},{24,16},{1,9},{9,1},{17,25},{25,17},{2,10},{10... | collective-permute-start | bytes 7077896 | tf_op jit(solution)/shard_map/ppermute | solution.py:353
  336.2 28.4 %collective-permute-start.7 = (bf16[8,96,768]{2,1,0:T(8,128)(2,1)S(1)}, bf16[8,96,768]{2,1,0:T(8,128)(2,1)S(1)}, u32[]{:S(2)}, u32[]{:S(2)}) collective-permute-start(bf16[8,96,768]{2,1,0:T(8,128)(2,1)S(1)} %fusion.21), channel_id=1, source_target_pairs={{0,16},{8,24},{16,0},{24,8},{1,17},{9,25},{17,1},{25,9},{2,18},{10... | collective-permute-start | bytes 3538952 | tf_op jit(solution)/shard_map/ppermute | solution.py:353
  367.8 38.9 %all-to-all-start.4 = ((bf16[8,96,768]{2,1,0:T(8,128)(2,1)}), bf16[8,96,768]{2,1,0:T(8,128)(2,1)}, u32[]{:S(2)}, u32[]{:S(2)}) async-start(bf16[8,96,768]{2,1,0:T(8,128)(2,1)} %fusion.23), calls=%async_computation.4 | async-start | bytes 2359296 | tf_op jit(solution)/shard_map/all_to_all | solution.py:375
  374.2 29.4 %copy-start.10 = (bf16[1,2,8,96,768]{4,3,2,1,0:T(8,128)(2,1)S(1)}, bf16[1,2,8,96,768]{4,3,2,1,0:T(8,128)(2,1)}, u32[]{:S(2)}) copy-start(bf16[1,2,8,96,768]{4,3,2,1,0:T(8,128)(2,1)} %maximum_bitcast_fusion) | copy-start | bytes 7077892
  376.2 27.4 %collective-permute-start.1 = (bf16[8,96,768]{2,1,0:T(8,128)(2,1)S(1)}, bf16[8,96,768]{2,1,0:T(8,128)(2,1)S(1)}, u32[]{:S(2)}, u32[]{:S(2)}) collective-permute-start(bf16[8,96,768]{2,1,0:T(8,128)(2,1)S(1)} %fusion.24), channel_id=1, source_target_pairs={{0,16},{8,24},{16,0},{24,8},{1,17},{9,25},{17,1},{25,9},{2,18},{10... | collective-permute-start | bytes 3538952 | tf_op jit(solution)/shard_map/ppermute | solution.py:353
  406.7 33.0 %all-to-all-start.2 = ((bf16[8,96,768]{2,1,0:T(8,128)(2,1)}), bf16[8,96,768]{2,1,0:T(8,128)(2,1)S(1)}, u32[]{:S(2)}, u32[]{:S(2)}) async-start(bf16[8,96,768]{2,1,0:T(8,128)(2,1)} %fusion.26), calls=%async_computation.2 | async-start | bytes 2359296 | tf_op jit(solution)/shard_map/all_to_all | solution.py:375
  420.6 23.7 %copy-start.39 = (s32[64]{0:T(128)S(1)}, s32[64]{0:T(128)}, u32[]{:S(2)}) copy-start(s32[64]{0:T(128)} %param.21) | copy-start | bytes 772
  440.7 42.4 %all-to-all-start.1 = ((bf16[2,32,16,768]{3,2,0,1:T(8,128)(2,1)}), bf16[2,32,16,768]{3,2,0,1:T(8,128)(2,1)S(1)}, u32[]{:S(2)}, u32[]{:S(2)}) async-start(bf16[2,32,16,768]{3,2,0,1:T(8,128)(2,1)} %copy.61), calls=%async_computation.1 | async-start | bytes 3145728 | tf_op jit(solution)/shard_map/all_to_all | solution.py:514
  445.3 1.2 collective-permute-start.4
  446.5 8.8 %collective-permute-start.5 = (f32[16,128]{1,0:T(8,128)S(1)}, f32[16,128]{1,0:T(8,128)S(1)}, u32[]{:S(2)}, u32[]{:S(2)}) collective-permute-start(f32[16,128]{1,0:T(8,128)S(1)} %add.258), channel_id=1, source_target_pairs={{0,16},{8,24},{16,0},{24,8},{1,17},{9,25},{17,1},{25,9},{2,18},{10... | collective-permute-start | bytes 24584 | tf_op jit(solution)/shard_map/ppermute | solution.py:353
  456.7 8.4 %collective-permute-start.2 = (bf16[96,768]{1,0:T(8,128)(2,1)S(1)}, bf16[96,768]{1,0:T(8,128)(2,1)S(1)}, u32[]{:S(2)}, u32[]{:S(2)}) collective-permute-start(bf16[96,768]{1,0:T(8,128)(2,1)S(1)} %reduce_sum.219), channel_id=1, source_target_pairs={{0,16},{8,24},{16,0},{24,8},{1,17},{9,25},{17,1},{25,9},{2,18},{10... | collective-permute-start | bytes 442376 | tf_op jit(solution)/shard_map/ppermute | solution.py:353
  457.8 27.1 %collective-permute-start.12 = (bf16[96,768]{1,0:T(8,128)(2,1)S(1)}, bf16[96,768]{1,0:T(8,128)(2,1)S(1)}, u32[]{:S(2)}, u32[]{:S(2)}) collective-permute-start(bf16[96,768]{1,0:T(8,128)(2,1)S(1)} %reduce_sum.231), channel_id=1, source_target_pairs={{0,16},{8,24},{16,0},{24,8},{1,17},{9,25},{17,1},{25,9},{2,18},{10... | collective-permute-start | bytes 442376 | tf_op jit(solution)/shard_map/ppermute | solution.py:353
  461.1 23.9 %collective-permute-start.8 = (bf16[96,768]{1,0:T(8,128)(2,1)S(1)}, bf16[96,768]{1,0:T(8,128)(2,1)S(1)}, u32[]{:S(2)}, u32[]{:S(2)}) collective-permute-start(bf16[96,768]{1,0:T(8,128)(2,1)S(1)} %reduce_sum.230), channel_id=1, source_target_pairs={{0,16},{8,24},{16,0},{24,8},{1,17},{9,25},{17,1},{25,9},{2,18},{10... | collective-permute-start | bytes 442376 | tf_op jit(solution)/shard_map/ppermute | solution.py:353
  465.1 20.5 %collective-permute-start.3 = (bf16[2,96,768]{2,1,0:T(8,128)(2,1)S(1)}, bf16[2,96,768]{2,1,0:T(8,128)(2,1)S(1)}, u32[]{:S(2)}, u32[]{:S(2)}) collective-permute-start(bf16[2,96,768]{2,1,0:T(8,128)(2,1)S(1)} %pad_maximum_fusion), channel_id=1, source_target_pairs={{0,8},{8,0},{16,24},{24,16},{1,9},{9,1},{17,25},{25,17},{2,10},{10... | collective-permute-start | bytes 884744 | tf_op jit(solution)/shard_map/ppermute | solution.py:353
  484.9 1.6 collective-permute-start.13
  485.1 2.5 collective-permute-start.9
  (19 other events, 58.6 us)
